TPU v7x, 32 devices: a whole 2x2x4 slice. The times are simulated.
32 devices in a mesh: tp: 4 (over z), dp: 8 (over y, x, core).
Axes of the slice: x: 2, y: 2, z: 4, core: 2. Of those that a mesh axis runs over, the one named last changes fastest.
Arguments:
- hidden: bfloat16 [8, 1024, 2048], P('dp')
- residual: float32 [8, 1024, 2048], P('dp')
- targets: int32 [8, 1024], P('dp')
- embedding: bfloat16 [50288, 2048], P('tp')
- norm_w: float32 [2048], replicated
Outputs:
- output 1: float32 [], replicated
- output 2: float32 [8, 1024, 2048], P('dp')
- output 3: float32 [50288, 2048], P('tp')
- output 4: float32 [2048], replicated
All inputs are finite; a program needn't handle non-finite values.
Results may differ from a plain program's by a relative error of at most 0.001.
Values sent between devices are 32-bit elements.
A program may use at most 1 GiB of HBM per device.

v0:
```python
import jax
import jax.numpy as jnp
from jax import lax
from jax.sharding import PartitionSpec as P

NORM_EPS = 1e-5


def solution(mesh):
    def program(hidden, residual, targets, embedding, norm_w):
        inv_n = 1.0 / (hidden.shape[0] * hidden.shape[1])

        def local_part(hid_loc, res_loc, tgt_loc, emb_loc, norm_vec):
            n_batch, n_seq, d_model = hid_loc.shape
            n_rows = n_batch * n_seq
            vocab_loc = emb_loc.shape[0]
            resid = (res_loc + hid_loc.astype(jnp.float32)).reshape(n_rows, d_model)
            tgt_rows = tgt_loc.reshape(n_rows)
            inv_rms = lax.rsqrt(jnp.mean(resid * resid, axis=-1, keepdims=True) + NORM_EPS)
            scaled_r = resid * inv_rms
            h_act = (scaled_r * norm_vec).astype(jnp.bfloat16)
            logits = jnp.einsum('td,vd->tv', h_act, emb_loc, preferred_element_type=jnp.float32)
            row_max = lax.pmax(jnp.max(logits, axis=-1, keepdims=True), 'tp')
            exp_shift = jnp.exp(logits - row_max)
            local_ids = tgt_rows - lax.axis_index('tp') * vocab_loc
            is_target = lax.broadcasted_iota(jnp.int32, (1, vocab_loc), 1) == local_ids[:, None]
            part_stats = jnp.stack([jnp.sum(exp_shift, axis=-1), jnp.sum(jnp.where(is_target, logits, 0.0), axis=-1)], axis=-1)
            tok_stats = lax.psum(part_stats, 'tp')
            sum_exp = tok_stats[:, 0:1]
            loss_part = jnp.sum(row_max[:, 0] + jnp.log(tok_stats[:, 0]) - tok_stats[:, 1]) * inv_n
            prob_rows = exp_shift / sum_exp
            dlogits = (jnp.where(is_target, prob_rows - 1.0, prob_rows) * inv_n).astype(jnp.bfloat16)
            grad_h = lax.psum(jnp.einsum('tv,vd->td', dlogits, emb_loc, preferred_element_type=jnp.float32), 'tp')
            grad_emb = lax.psum(jnp.einsum('tv,td->vd', dlogits, h_act, preferred_element_type=jnp.float32), 'dp')
            grad_scaled = grad_h * norm_vec
            grad_r = inv_rms * (grad_scaled - scaled_r * jnp.mean(grad_scaled * scaled_r, axis=-1, keepdims=True))
            grad_w, loss_mean = lax.psum((jnp.sum(grad_h * scaled_r, axis=0), loss_part), 'dp')
            return loss_mean, grad_r.reshape(n_batch, n_seq, d_model), grad_emb, grad_w

        sharded = jax.shard_map(
            local_part, mesh=mesh,
            in_specs=(P('dp', None, None), P('dp', None, None), P('dp', None), P('tp', None), P(None)),
            out_specs=(P(), P('dp', None, None), P('tp', None), P(None)),
            check_vma=False)
        return sharded(hidden, residual, targets, embedding, norm_w)

    return program
```

profile of v0, /device:TPU:1, one launch (start us, length us, event | category | flops | bytes accessed | tf_op | source)
XLA Modules:
  0.0 1728.2 jit_solution(17633910900016004775)
XLA Ops:
  7.2 0.0 all-reduce.4.cloned.1.call-start
  7.2 0.0 copy-start.5
  7.2 5.7 fusion.3
  13.0 0.0 copy-start
  13.0 0.0 copy-done.5
  13.0 0.0 copy-start.7
  13.0 66.9 %fusion.7 = (f32[1024]{0:T(1024)S(1)}, f32[1024,12572]{0,1:T(8,128)}) fusion(bf16[12572,2048]{1,0:T(8,128)(2,1)} %param.8, f32[1,1024,2048]{2,1,0:T(8,128)S(1)} %get-tuple-element.11, f32[2048]{0:T(1024)S(1)} %copy-done.5, f32[1024]{0:T(1024)S(1)} %add_rsqrt_fusion), kind=kOutput, calls=%fused_computation.23 | convolution fusion | flops 52749955072 | bytes 111394816 | tf_op jit(solution)/shard_map/td,vd->tv/dot_general | solution.py:22
  79.9 0.0 copy-done
  79.9 10.8 pmax.7
  90.7 0.0 copy-start.1
  90.7 0.0 copy-done.7
  90.7 22.3 %fusion.2 = (f32[1024]{0:T(1024)S(1)}, f32[1024]{0:T(1024)S(1)}) fusion(f32[1024,12572]{0,1:T(8,128)} %get-tuple-element.15, f32[1024]{0:T(1024)S(1)} %pmax.7, s32[1024]{0:T(1024)S(1)} %bitcast.34), kind=kLoop, calls=%fused_computation.6 | loop fusion | flops 64366592 | bytes 51511296 | tf_op jit(solution)/shard_map/reduce_sum | solution.py:27
  113.1 7.0 psum.35
  120.0 0.6 fusion.6
  120.6 0.0 copy-done.1
  120.6 26.7 %fusion.1 = bf16[1024,12572]{0,1:T(8,128)(2,1)} fusion(f32[1024,12572]{0,1:T(8,128)} %get-tuple-element.15, f32[1024]{0:T(1024)S(1)} %bitcast.36, s32[1024]{0:T(1024)S(1)} %bitcast.35, f32[1024]{0:T(1024)S(1)} %pmax.7), kind=kLoop, calls=%fused_computation.2 | loop fusion | flops 90116096 | bytes 77254656 | tf_op jit(solution)/shard_map/convert_element_type | solution.py:32
  147.3 0.0 copy-done.3
  147.3 63.6 %fusion.8 = f32[1024,2048]{1,0:T(8,128)} fusion(bf16[1024,12572]{0,1:T(8,128)(2,1)} %fusion.1, bf16[12572,2048]{1,0:T(8,128)(2,1)} %param.8), kind=kOutput, calls=%fused_computation.24 | convolution fusion | flops 52730789888 | bytes 85630976 | tf_op jit(solution)/shard_map/tv,vd->td/dot_general | solution.py:33
  211.0 0.0 all-reduce.4.cloned.1.call-update
  211.0 0.3 all-reduce.6.cloned.1.call-start
  211.3 65.8 %fusion.4 = f32[12572,2048]{1,0:T(8,128)} fusion(bf16[1024,12572]{0,1:T(8,128)(2,1)} %fusion.1, f32[1,1024,2048]{2,1,0:T(8,128)} %copy-done, f32[2048]{0:T(1024)S(1)} %copy-done.5, f32[1024]{0:T(1024)S(1)} %add_rsqrt_fusion), kind=kOutput, calls=%fused_computation.20 | convolution fusion | flops 52737081344 | bytes 137138176 | tf_op jit(solution)/shard_map/tv,td->vd/dot_general | solution.py:34
  277.1 0.0 all-reduce.6.cloned.1.call-update
  277.1 0.6 copy-done.2
  277.8 0.0 copy-done.4
  277.8 0.0 copy-done.6
  277.8 0.6 subtract_reduce_fusion
  279.0 223.9 %all-reduce.4.cloned.1.call-done = f32[1024,2048]{1,0:T(8,128)} async-done(((f32[1024,2048]{1,0:T(8,128)}), f32[1024,2048]{1,0:T(8,128)}) %all-reduce.4.cloned.1.call-update) | async-done | bytes 8388624 | tf_op jit(solution)/shard_map/psum | solution.py:33
  503.0 6.9 multiply_reduce_fusion
  509.9 14.1 all-reduce
  524.0 10.0 multiply_bitcast_fusion
  534.0 1119.6 %all-reduce.6.cloned.1.call-done = f32[12572,2048]{1,0:T(8,128)} async-done(((f32[12572,2048]{1,0:T(8,128)}), f32[12572,2048]{1,0:T(8,128)}) %all-reduce.6.cloned.1.call-update) | async-done | bytes 102989840 | tf_op jit(solution)/shard_map/psum | solution.py:34
  1653.6 67.8 %copy.11 = f32[12572,2048]{1,0:T(8,128)} copy(f32[12572,2048]{1,0:T(8,128)} %all-reduce.6.cloned.1.call-done) | data formatting | bytes 205979648
  (8 shorter events, 0.0 us)
Async XLA Ops:
  7.2 495.8 %all-reduce.4.cloned.1.call-start = ((), (), s32[]{:S(2)}) async-start(), calls=%async_computation | async-start | bytes 16777216 | tf_op jit(solution)/shard_map/psum | solution.py:33
  7.2 5.8 copy-start.5
  13.0 67.0 %copy-start = (f32[1,1024,2048]{2,1,0:T(8,128)}, f32[1,1024,2048]{2,1,0:T(8,128)S(1)}, u32[]{:S(2)}) copy-start(f32[1,1024,2048]{2,1,0:T(8,128)S(1)} %get-tuple-element.11) | copy-start | bytes 25165828
  13.0 77.7 %copy-start.7 = (s32[1,1024]{1,0:T(1,128)S(1)}, s32[1,1024]{1,0:T(1,128)}, u32[]{:S(2)}) copy-start(s32[1,1024]{1,0:T(1,128)} %param.7) | copy-start | bytes 12292
  90.7 29.9 %copy-start.1 = (f32[1024]{0:T(1024)}, f32[1024]{0:T(1024)S(1)}, u32[]{:S(2)}) copy-start(f32[1024]{0:T(1024)S(1)} %pmax.7) | copy-start | bytes 12292
  120.6 26.7 %copy-start.3 = (f32[1024,1]{0,1:T(1,128)}, f32[1024,1]{0,1:T(1,128)S(1)}, u32[]{:S(2)}) copy-start(f32[1024,1]{0,1:T(1,128)S(1)} %get-tuple-element.12) | copy-start | bytes 12292
  211.0 1442.6 %all-reduce.6.cloned.1.call-start = ((), (), s32[]{:S(2)}) async-start(), calls=%async_computation.1 | async-start | bytes 206045184 | tf_op jit(solution)/shard_map/psum | solution.py:34
  277.1 0.7 copy-start.2
  277.1 0.7 copy-start.4
  277.1 0.7 copy-start.6
Sparse Core Ops, SparseCore 0:
  211.1 291.8 all-reduce.3
  507.3 1146.2 all-reduce.5
where the time goes:
time: 1730 us
  waiting for transfers between devices  1340 us (77%)
  matrix products  196 us (11%)
  other arithmetic  72.3 us (4%)
  local copies, waits for them, and re-layouts  69.1 us (4%)
  blocking collectives  31.8 us (2%)
    psum x1, waiting for transfers between devices, local_part(): lax.psum(jnp.einsum('tv,td->vd', dlogits, h_act, preferred_element_type=j...  1120 us
    psum x1, waiting for transfers between devices, local_part(): lax.psum(jnp.einsum('tv,vd->td', dlogits, emb_loc, preferred_element_type...  224 us
    unnamed x17, local copies, waits for them, and re-layouts  68.5 us
    dot_general x1, matrix products, local_part(): jnp.einsum('td,vd->tv', h_act, emb_loc, preferred_element_type=jnp.float32)  66.9 us
    dot_general x1, matrix products, local_part(): jnp.einsum('tv,td->vd', dlogits, h_act, preferred_element_type=jnp.float32)  65.8 us
    dot_general x1, matrix products, local_part(): jnp.einsum('tv,vd->td', dlogits, emb_loc, preferred_element_type=jnp.floa...  63.6 us
  transfers between devices with their start and end apart: 2, of which 2 were waited for; matrix products, arithmetic and copies ran while one was open for 5% of the time, Pallas kernels for 0%

commit v1 on v0

v1 whole, which is shorter than its diff:
```python
import functools

import jax
import jax.numpy as jnp
from jax import lax
from jax.experimental import pallas as pl
from jax.experimental.pallas import tpu as pltpu
from jax.sharding import PartitionSpec as P


EPS = 1e-5
NEG = -3.0e38
VMEM_CAP = 66 * 1024 * 1024
NT = (((1,), (1,)), ((), ()))
NN = (((1,), (0,)), ((), ()))
TN = (((0,), (0,)), ((), ()))
VB = 1280
SUB = 256
TB = 128
R = 704
NF = 5
GROUPS = (2, 2, 1)


def params(**kw):
    return pltpu.CompilerParams(vmem_limit_bytes=VMEM_CAP, **kw)


def cost(flops, nbytes, exps=0):
    return pl.CostEstimate(flops=int(flops), bytes_accessed=int(nbytes), transcendentals=int(exps))


def whole(shape):
    return pl.BlockSpec(shape, lambda *a: (0,) * len(shape), pipeline_mode=pl.Buffered(1))


def norm_body(hid_ref, res_ref, w_ref, *refs):
    hb_ref, inv_ref, hf_ref = refs[-3:]
    r = res_ref[...] + hid_ref[...].astype(jnp.float32)
    inv = lax.rsqrt(jnp.mean(r * r, axis=-1, keepdims=True) + EPS)
    h = (r * inv * w_ref[...]).astype(jnp.bfloat16)
    hb_ref[...] = h
    hf_ref[...] = h.astype(jnp.float32)
    inv_ref[...] = inv


def norm_fwd(hid, res, w, half, so_far=()):
    n, d = hid.shape
    steps = n // (2 * TB)
    src = pl.BlockSpec((TB, d), lambda i: (i + half * steps, 0))
    return pl.pallas_call(
        norm_body, grid=(steps,),
        out_shape=(jax.ShapeDtypeStruct((n, d), jnp.bfloat16), jax.ShapeDtypeStruct((n, 1), jnp.float32),
                   jax.ShapeDtypeStruct((n // 2, d), jnp.float32)),
        in_specs=[src, src, whole((1, d))] + [pl.BlockSpec(memory_space=pl.ANY)] * len(so_far),
        out_specs=[src, pl.BlockSpec((TB, 1), lambda i: (i + half * steps, 0)), pl.BlockSpec((TB, d), lambda i: (i, 0))],
        input_output_aliases={3: 0, 4: 1} if so_far else {},
        cost_estimate=cost(8 * n * d, 6 * n * d), compiler_params=params(), name="norm_fwd")(hid, res, w, *so_far)


def fwd_body(vocab, h_ref, e_ref, lg_ref, st_ref, m_scr, s_scr):
    i = pl.program_id(0)
    n = h_ref.shape[0]

    @pl.when(i == 0)
    def _():
        m_scr[...] = jnp.full_like(m_scr, NEG)
        s_scr[...] = jnp.zeros_like(s_scr)

    def dot(k):
        return lax.dot_general(e_ref[pl.ds(k * SUB, SUB), :], h_ref[...], NT, preferred_element_type=jnp.float32)

    def stats(l, k):
        if (k + 1) * SUB > vocab % VB:
            row = lax.broadcasted_iota(jnp.int32, (SUB, 1), 0)
            l = jnp.where(row < vocab - i * VB - k * SUB, l, NEG)
        lg_ref[pl.ds(k * SUB, SUB), :] = l
        m_old = m_scr[...]
        l = l.reshape(SUB // 8, 8, n)
        m_new = jnp.maximum(m_old, jnp.max(l, axis=0))
        m_scr[...] = m_new
        s_scr[...] = s_scr[...] * jnp.exp(m_old - m_new) + jnp.sum(jnp.exp(l - m_new[None]), axis=0)

    l = dot(0)
    for k in range(VB // SUB):
        after = dot(k + 1) if (k + 1) * SUB < VB else None
        stats(l, k)
        l = after

    @pl.when(i == pl.num_programs(0) - 1)
    def _():
        m = m_scr[...]
        mx = jnp.max(m, axis=0, keepdims=True)
        sm = jnp.sum(s_scr[...] * jnp.exp(m - mx), axis=0, keepdims=True)
        row = lax.broadcasted_iota(jnp.int32, (8, 1), 0)
        st_ref[...] = jnp.where(row == 0, mx, sm)


def forward(h, emb):
    n, d = h.shape
    vocab = emb.shape[0]
    nb = pl.cdiv(vocab, VB)
    return pl.pallas_call(
        functools.partial(fwd_body, vocab), grid=(nb,),
        out_shape=(jax.ShapeDtypeStruct((nb * VB, n), jnp.float32), jax.ShapeDtypeStruct((8, n), jnp.float32)),
        in_specs=[whole((n, d)), pl.BlockSpec((VB, d), lambda i: (i, 0))],
        out_specs=[pl.BlockSpec((VB, n), lambda i: (i, 0)), pl.BlockSpec((8, n), lambda i: (0, 0))],
        scratch_shapes=[pltpu.VMEM((8, n), jnp.float32)] * 2,
        cost_estimate=cost(2 * n * d * vocab, 2 * vocab * d + 4 * n * vocab, n * vocab),
        compiler_params=params(), name="forward")(h, emb)


def dh_body(vocab, inv_n, lg_ref, e_ref, st_ref, inv_ref, hid_ref, res_ref, dh_ref, t_ref, hid_scr, res_scr, t_scr, sem):
    i = pl.program_id(0)
    n = st_ref.shape[1]
    loads = [pltpu.make_async_copy(hid_ref, hid_scr, sem.at[0]), pltpu.make_async_copy(res_ref, res_scr, sem.at[1])]

    @pl.when(i == 0)
    def _():
        for c in loads:
            c.start()
        dh_ref[...] = jnp.zeros_like(dh_ref)
        t_scr[...] = jnp.zeros_like(t_scr)

    m, si = st_ref[0:1], st_ref[1:2]
    row = lax.broadcasted_iota(jnp.int32, (SUB, 1), 0)
    rowf = row.astype(jnp.float32)

    def dlogits(k):
        l = lg_ref[pl.ds(k * SUB, SUB), :]
        p = jnp.exp(l - m) * si
        hit = rowf == st_ref[2:3] - (i * VB + k * SUB).astype(jnp.float32)
        t = t_scr[...]
        for u in range(SUB // 8):
            t = jnp.where(hit[u * 8:(u + 1) * 8], l[u * 8:(u + 1) * 8], t)
        t_scr[...] = t
        return jnp.where(hit, p - inv_n, p).astype(jnp.bfloat16)

    g = dlogits(0)
    for k in range(VB // SUB):
        after = dlogits(k + 1) if (k + 1) * SUB < VB else None
        e = e_ref[pl.ds(k * SUB, SUB), :]
        if (k + 1) * SUB > vocab % VB:
            e = jnp.where(row < vocab - i * VB - k * SUB, e, 0)
        dh_ref[pl.ds(0, n), :] += lax.dot_general(g, e, TN, preferred_element_type=jnp.float32)
        g = after

    @pl.when(i == pl.num_programs(0) - 1)
    def _():
        for c in loads:
            c.wait()
        t_ref[...] = t_scr[...]
        acc = jnp.zeros((8, dh_ref.shape[1]), jnp.float32)
        for q in range(n // TB):
            rows = pl.ds(q * TB, TB)
            v = dh_ref[rows, :] * ((res_scr[rows, :] + hid_scr[rows, :].astype(jnp.float32)) * inv_ref[rows, :])
            for u in range(TB // 8):
                acc = acc + v[u * 8:(u + 1) * 8]
        dh_ref[pl.ds(n, 8), :] = acc


def backward_h(lg, emb, st, inv, hid, res, inv_n):
    n, d = hid.shape
    vocab = emb.shape[0]
    any_space = pl.BlockSpec(memory_space=pl.ANY)
    return pl.pallas_call(
        functools.partial(dh_body, vocab, inv_n), grid=(lg.shape[0] // VB,),
        out_shape=(jax.ShapeDtypeStruct((n + 8, d), jnp.float32), jax.ShapeDtypeStruct((8, n), jnp.float32)),
        in_specs=[pl.BlockSpec((VB, n), lambda i: (i, 0)), pl.BlockSpec((VB, d), lambda i: (i, 0)), whole((8, n)), whole((n, 1)),
                  any_space, any_space],
        out_specs=[whole((n + 8, d)), pl.BlockSpec((8, n), lambda i: (0, 0))],
        scratch_shapes=[pltpu.VMEM((n, d), jnp.bfloat16), pltpu.VMEM((n, d), jnp.float32), pltpu.VMEM((8, n), jnp.float32),
                        pltpu.SemaphoreType.DMA((2,))],
        cost_estimate=cost(2 * n * d * vocab, 2 * vocab * d + 4 * n * vocab, n * vocab),
        compiler_params=params(), name="backward_h")(lg, emb, st, inv, hid, res)


def resid_body(dh_ref, hid_ref, res_ref, inv_ref, w_ref, out_ref):
    inv = inv_ref[...]
    nrm = (res_ref[...] + hid_ref[...].astype(jnp.float32)) * inv
    dn = dh_ref[...] * w_ref[...]
    out_ref[...] = inv * (dn - nrm * jnp.mean(dn * nrm, axis=-1, keepdims=True))


def resid_grad(dh, hid, res, inv, w):
    n, d = hid.shape
    blk = pl.BlockSpec((TB, d), lambda i: (i, 0))
    return pl.pallas_call(
        resid_body, grid=(n // TB,), out_shape=jax.ShapeDtypeStruct((n, d), jnp.float32),
        in_specs=[blk, blk, blk, pl.BlockSpec((TB, 1), lambda i: (i, 0)), whole((1, d))], out_specs=blk,
        cost_estimate=cost(8 * n * d, 14 * n * d), compiler_params=params(), name="resid_grad")(dh, hid, res, inv, w)


def dlogits(l, st, base, inv_n):
    row = lax.broadcasted_iota(jnp.int32, (l.shape[0], 1), 0).astype(jnp.float32)
    p = jnp.exp(l - st[0:1]) * st[1:2]
    return jnp.where(row == st[2:3] - base, p - inv_n, p).astype(jnp.bfloat16)


def nt(a, b):
    return lax.dot_general(a, b, NT, preferred_element_type=jnp.float32)


def nn(a, b):
    return lax.dot_general(a, b, NN, preferred_element_type=jnp.float32)


def plane_rows_body(np_, own, split, inv_n, off_ref, e_ref, st_ref, *refs):
    if own:
        lg_ref, hb_ref, refs = refs[0], refs[1], refs[2:]
    else:
        acc_ref, refs = refs[0], refs[2:]
    h_refs, refs = refs[:2 * np_], refs[2 * np_:]
    out_refs, refs = refs[:split], refs[split:]
    all_ref, buf, h_scr, sem = refs
    i = pl.program_id(0)
    half = buf.shape[1] // 2

    def load(k, slot):
        return [pltpu.make_async_copy(h_refs[2 * k + u], buf.at[slot, pl.ds(u * half, half)], sem.at[slot, u]) for u in range(2)]

    @pl.when(i == 0)
    def _():
        for c in load(0, 0):
            c.start()

    for k in range(1, np_):
        @pl.when(i + 1 == k)
        def _():
            for c in load(k, k % 2):
                c.start()

    base = off_ref[0].astype(jnp.float32)
    rh = R // 2

    @pl.when(i == 0)
    def _():
        for u in range(2):
            o, at = out_refs[u % split], 0 if split == 2 else u * rh
            if own:
                o[pl.ds(at, rh), :] = nn(dlogits(lg_ref[pl.ds(u * rh, rh), :], st_ref[0], base + u * rh, inv_n), hb_ref[...])
            else:
                o[pl.ds(at, rh), :] = acc_ref[pl.ds(u * rh, rh), :]

    slot = lax.rem(i, 2)
    for u in range(2):
        pltpu.make_async_copy(h_refs[u], buf.at[slot, pl.ds(u * half, half)], sem.at[slot, u]).wait()
    h_scr[...] = buf[slot].astype(jnp.bfloat16)
    all_ref[...] = h_scr[...]

    st = st_ref[i + own]
    ls = [nt(e_ref[pl.ds(u * rh, rh), :], h_scr[...]) for u in range(2)]
    for u in range(2):
        o, at = out_refs[u % split], 0 if split == 2 else u * rh
        o[pl.ds(at, rh), :] += nn(dlogits(ls[u], st, base + u * rh, inv_n), h_scr[...])


def plane_rows(off, emb, st, parts, inv_n, split, slots, own=None, acc=None, so_far=None):
    np_, (half, d) = len(parts) // 2, parts[0].shape
    n = 2 * half
    one = pl.Buffered(1)
    at = lambda i, off: (pl.multiple_of(off[0], 16), 0)
    whole_r = lambda r: pl.BlockSpec((r, d), lambda i, off: (0, 0), pipeline_mode=one)
    any_space = pl.BlockSpec(memory_space=pl.ANY)
    if own is not None:
        lead, specs = list(own), [pl.BlockSpec((pl.Element(R), pl.Element(n)), at, pipeline_mode=one), whole((n, d))]
    else:
        lead, specs = [acc, so_far], [whole_r(R), any_space]
    return pl.pallas_call(
        functools.partial(plane_rows_body, np_, int(own is not None), split, inv_n),
        out_shape=tuple([jax.ShapeDtypeStruct((R // split, d), jnp.float32)] * split + [jax.ShapeDtypeStruct((7, n, d), jnp.bfloat16)]),
        grid_spec=pltpu.PrefetchScalarGridSpec(
            num_scalar_prefetch=1, grid=(np_,),
            in_specs=[pl.BlockSpec((pl.Element(R, (0, R)), pl.Element(d)), at, pipeline_mode=one), whole(st.shape)] + specs
            + [any_space] * (2 * np_),
            out_specs=tuple([whole_r(R // split)] * split + [pl.BlockSpec((None, n, d), lambda i, off: (slots(i), 0, 0))]),
            scratch_shapes=[pltpu.VMEM((2, n, d), jnp.float32), pltpu.VMEM((n, d), jnp.bfloat16), pltpu.SemaphoreType.DMA((2, 2))]),
        input_output_aliases={} if own is not None else {4: split},
        cost_estimate=cost(4 * np_ * n * d * R, 6 * np_ * n * d, np_ * n * R),
        compiler_params=params(), name="plane_rows")(off, emb, st, *lead, *parts)


def chip_rows(off, lg, emb, st, hb, hs, slot, nb, inv_n):
    n, d = hb.shape

    def body(off_ref, lg_ref, e_ref, st_ref, h_ref, s_ref, out_ref):
        base = off_ref[1 + pl.program_id(0)].astype(jnp.float32)
        l = nt(e_ref[...], s_ref[...])
        out_ref[...] = nn(dlogits(lg_ref[...], st_ref[0], base, inv_n), h_ref[...])
        out_ref[...] += nn(dlogits(l, st_ref[1], base, inv_n), s_ref[...])

    at = lambda i, off: (pl.multiple_of(off[1 + i], 16), 0)
    return pl.pallas_call(
        body, out_shape=jax.ShapeDtypeStruct((nb * R, d), jnp.float32),
        grid_spec=pltpu.PrefetchScalarGridSpec(
            num_scalar_prefetch=1, grid=(nb,),
            in_specs=[pl.BlockSpec((pl.Element(R), pl.Element(n)), at), pl.BlockSpec((pl.Element(R, (0, R)), pl.Element(d)), at),
                      whole((8, 8, n)), whole((n, d)), pl.BlockSpec((None, n, d), lambda i, off: (slot, 0, 0), pipeline_mode=pl.Buffered(1))],
            out_specs=pl.BlockSpec((R, d), lambda i, off: (i, 0))),
        cost_estimate=cost(6 * n * d * nb * R, 8 * d * nb * R, 2 * n * nb * R),
        compiler_params=params(), name="chip_rows")(off, lg, emb, st, hb, hs)


def rest_rows(off, b0, nb, ng, emb, st, acc, hs, inv_n):
    n, d = hs.shape[1], hs.shape[2]

    def body(off_ref, e_ref, st_ref, h_ref, acc_ref, out_ref):
        i, j = pl.program_id(0), pl.program_id(1)
        base = off_ref[1 + b0 + i].astype(jnp.float32)
        l = nt(e_ref[...], h_ref[0])
        for q in range(2):
            after = nt(e_ref[...], h_ref[1]) if q == 0 else None
            x = nn(dlogits(l, st_ref[q], base, inv_n), h_ref[q])
            if q == 0:
                out_ref[...] = jnp.where(j == 0, acc_ref[...], out_ref[...]) + x
            else:
                out_ref[...] += x
            l = after

    return pl.pallas_call(
        body, out_shape=jax.ShapeDtypeStruct((nb * R, d), jnp.float32),
        grid_spec=pltpu.PrefetchScalarGridSpec(
            num_scalar_prefetch=1, grid=(nb, ng),
            in_specs=[pl.BlockSpec((pl.Element(R, (0, R)), pl.Element(d)), lambda i, j, off: (pl.multiple_of(off[1 + b0 + i], 16), 0)),
                      pl.BlockSpec((2, 8, n), lambda i, j, off: (j + 1, 0, 0)), pl.BlockSpec((2, n, d), lambda i, j, off: (j, 0, 0)),
                      pl.BlockSpec((R, d), lambda i, j, off: (b0 + i, 0))],
            out_specs=pl.BlockSpec((R, d), lambda i, j, off: (i, 0))),
        cost_estimate=cost(4 * 2 * ng * n * d * nb * R, 10 * d * nb * R, 2 * ng * n * nb * R),
        compiler_params=params(), name="rest_rows")(off, emb, st, hs, acc)


NBUF = 8
CH = 200


def place_body(jobs, pos_ref, *refs):
    srcs, out_ref, buf, isem, osem = refs[:-4], refs[-4], refs[-3], refs[-2], refs[-1]
    n = len(jobs)

    def fetch(j):
        s, r0, rows, _, _, _ = jobs[j]
        return pltpu.make_async_copy(srcs[s].at[pl.ds(r0, rows)], buf.at[j % NBUF, pl.ds(0, rows)], isem.at[j % NBUF])

    def put(j, rows):
        _, _, _, k, add, _ = jobs[j]
        at = pl.multiple_of(pos_ref[k] + add, 8)
        return pltpu.make_async_copy(buf.at[j % NBUF, pl.ds(0, rows)], out_ref.at[pl.ds(at, rows)], osem.at[j % NBUF])

    def each(j, f):
        _, _, rows, k, _, short = jobs[j]
        if short == rows:
            f(put(j, rows))
        else:
            last = pos_ref[k] == pos_ref[0]

            @pl.when(last)
            def _():
                if short > 0:
                    f(put(j, short))

            @pl.when(jnp.logical_not(last))
            def _():
                f(put(j, rows))

    lead = NBUF // 2
    for j in range(min(lead, n)):
        fetch(j).start()
    for j in range(n):
        fetch(j).wait()
        each(j, lambda c: c.start())
        nxt = j + lead
        if nxt < n:
            if nxt >= NBUF:
                each(nxt - NBUF, lambda c: c.wait())
            fetch(nxt).start()
    for j in range(max(0, n - NBUF), n):
        each(j, lambda c: c.wait())


def place(pos, pieces, vocab, d, tail, so_far=None):
    jobs, ops = [], []
    for arr, k, add, ends in pieces:
        ops.append(arr)
        for r0 in range(0, arr.shape[0], CH):
            rows = min(CH, arr.shape[0] - r0)
            short = max(0, min(rows, (tail - add - r0) // 8 * 8)) if ends else rows
            jobs.append((len(ops) - 1, r0, rows, k, add + r0, short))
    if so_far is not None:
        ops.append(so_far)
    return pl.pallas_call(
        functools.partial(place_body, jobs), out_shape=jax.ShapeDtypeStruct((vocab, d), jnp.float32),
        input_output_aliases={} if so_far is None else {len(ops): 0},
        grid_spec=pltpu.PrefetchScalarGridSpec(
            num_scalar_prefetch=1, grid=(), in_specs=[pl.BlockSpec(memory_space=pl.ANY)] * len(ops),
            out_specs=pl.BlockSpec(memory_space=pl.ANY),
            scratch_shapes=[pltpu.VMEM((NBUF, CH, d), jnp.float32), pltpu.SemaphoreType.DMA((NBUF,)), pltpu.SemaphoreType.DMA((NBUF,))]),
        cost_estimate=cost(1000, 8 * vocab * d), compiler_params=params(), name="place")(pos, *ops)


def place_tail(pos, own, other, row, out):
    vocab, d = out.shape

    def body(pos_ref, own_ref, other_ref, _, out_ref):
        out_ref[...] = jnp.where(pos_ref[9] == pos_ref[0], own_ref[...], other_ref[...])

    src = pl.BlockSpec((8, d), lambda i, pos: (row // 8, 0))
    return pl.pallas_call(
        body, out_shape=jax.ShapeDtypeStruct((vocab, d), jnp.float32),
        grid_spec=pltpu.PrefetchScalarGridSpec(
            num_scalar_prefetch=1, grid=(1,), in_specs=[src, src, pl.BlockSpec(memory_space=pl.ANY)],
            out_specs=pl.BlockSpec((8, d), lambda i, pos: (vocab // 8, 0))),
        input_output_aliases={3: 0}, compiler_params=params(), name="place_tail")(pos, own, other, out)


def solution(mesh):
    n_dp = mesh.shape['dp']

    def hop(dx, dy, dc):
        perm = []
        for i in range(n_dp):
            c, x, y = i % 2, (i // 2) % 2, i // 4
            perm.append((i, ((y ^ dy) * 2 + (x ^ dx)) * 2 + (c ^ dc)))
        return lambda a: lax.ppermute(a, 'dp', perm)

    over_x, over_y, over_c = hop(1, 0, 0), hop(0, 1, 0), hop(0, 0, 1)

    def program(hidden, residual, targets, embedding, norm_w):
        n_tok = hidden.shape[0] * hidden.shape[1]
        inv_n = 1.0 / n_tok

        def body(hid_loc, res_loc, tgt_loc, emb, norm_vec):
            _, n, d = hid_loc.shape
            hid, res = hid_loc.reshape(n, d), res_loc.reshape(n, d)
            vocab = emb.shape[0]
            w = norm_vec.reshape(1, d)
            tp, dp = lax.axis_index('tp'), lax.axis_index('dp')
            hb, inv, hf1 = norm_fwd(hid, res, w, 0)
            x1 = over_x(hf1)
            hb, inv, hf2 = norm_fwd(hid, res, w, 1, (hb, inv))
            y2 = over_y(hf2)
            x2, y1, s1, s2 = over_x(hf2), over_y(hf1), over_c(hf1), over_c(hf2)
            d1, d2 = over_y(x1), over_x(y2)
            xs1, ys2 = over_c(x1), over_c(y2)
            xs2, ys1 = over_c(x2), over_c(y1)
            ds1, ds2 = over_c(d1), over_c(d2)
            lg, st = forward(hb, emb)
            st = lax.all_gather(st[0:2], 'tp', axis=0)
            mx = jnp.max(st[:, 0], axis=0)
            sm = jnp.sum(st[:, 1] * jnp.exp(st[:, 0] - mx), axis=0)
            tgt = tgt_loc.reshape(n) - tp * vocab
            tgt = jnp.where((tgt >= 0) & (tgt < vocab), tgt, -1).astype(jnp.float32)
            mine = jnp.concatenate([jnp.stack([mx, inv_n / sm, tgt]), jnp.zeros((5, n), jnp.float32)], axis=0)
            dhg, hit = backward_h(lg, emb, mine, inv, hid, res, inv_n)
            own_loss = jnp.where(tp == 0, jnp.sum(mx + jnp.log(sm)), 0.0) - jnp.sum(hit)
            extra = jnp.concatenate([jnp.sum(dhg[n:], axis=0), jnp.full((n,), own_loss * inv_n)]).reshape(3, n)
            plane = lax.all_gather(jnp.concatenate([mine[0:3], extra, mine[6:8]], axis=0), 'dp', axis=0)
            sums = jnp.sum(plane[:, 3:6], axis=0).reshape(3 * n)
            top = jnp.concatenate([jnp.stack([sums[:d], jnp.broadcast_to(sums[2 * n], (d,))]), jnp.zeros((6, d), jnp.float32)], axis=0)
            dhg = lax.psum(lax.dynamic_update_slice(dhg, top, (n, 0)), 'tp')
            grad_w, loss = dhg[n], dhg[n + 1, 0]
            order = jnp.stack([dp ^ k for k in range(n_dp)])
            plane = plane[order]

            f0 = n_dp * R
            fh = NF * R
            core = dp % 2
            off = jnp.concatenate([jnp.stack([dp * R]), f0 + core * fh + R * jnp.arange(NF)]).astype(jnp.int32)
            gate = lax.optimization_barrier
            a, hs = plane_rows(off, emb, plane, [s1, s2, x1, x2, xs1, xs2, y1, y2, ys1, ys2], inv_n, 1, lambda i: lax.rem(i + 6, 7), own=(lg, hb))
            acc = chip_rows(off, lg, emb, plane, hb, hs, 6, NF, inv_n)
            a, _ = gate((a, acc))
            a1, a2, hs = plane_rows(off, emb, plane[6:8], [d1, d2, ds1, ds2], inv_n, 2, lambda i: i + 4, acc=a, so_far=hs)
            ax1, ay2 = over_x(a1), over_y(a2)
            ax2, ay1 = over_x(a2), over_y(a1)
            as1, as2 = over_c(a1), over_c(a2)
            ad1, ad2 = over_y(ax1), over_x(ay2)
            axs1, ays2 = over_c(ax1), over_c(ay2)
            axs2, ays1 = over_c(ax2), over_c(ay1)
            ads1, ads2 = over_c(ad1), over_c(ad2)
            pieces, last, j = [], a1, 0
            for k, (p1, p2) in enumerate([(a1, a2), (as1, as2), (ax1, ax2), (axs1, axs2), (ay1, ay2), (ays1, ays2), (ad1, ad2), (ads1, ads2)]):
                pieces += [(p1, 1 + k, 0, False), (p2, 1 + k, R // 2, False)]
            tail = vocab - f0 - fh
            for cnt in GROUPS:
                acc, last = gate((acc, last))
                last = rest_rows(off, j, cnt, 3, emb, plane, acc, hs, inv_n)
                other = over_c(last)
                pieces = [(last, 9, j * R, True), (other, 10, j * R, True)] + pieces
                if j * R <= tail < (j + cnt) * R:
                    ending = (last, other, tail // 8 * 8 - j * R)
                j += cnt
            pos = jnp.concatenate([jnp.stack([f0 + fh]), order * R, jnp.stack([f0 + core * fh, f0 + (1 - core) * fh])]).astype(jnp.int32)
            late = [p for p in pieces if p[0] is ads1 or p[0] is ads2 or p[0] is other]
            grad_emb = place(pos, [p for p in pieces if all(p[0] is not q[0] for q in late)], vocab, d, tail)
            grad_emb = place(pos, late, vocab, d, tail, grad_emb)
            if vocab % 8:
                grad_emb = place_tail(pos, *ending, grad_emb)
            grad_r = resid_grad(dhg, hid, res, inv, w)
            return loss, grad_r.reshape(hid_loc.shape), grad_emb, grad_w

        sharded = jax.shard_map(
            body, mesh=mesh,
            in_specs=(P('dp', None, None), P('dp', None, None), P('dp', None), P('tp', None), P(None)),
            out_specs=(P(), P('dp', None, None), P('tp', None), P(None)),
            check_vma=False)
        return sharded(hidden, residual, targets, embedding, norm_w)

    return program
```

time: 1730 us -> 1070 us (0.62)
  waiting for transfers between devices: 1340 us -> 417 us
  Pallas kernels: 0 us -> 569 us
  matrix products: 196 us -> 0 us
  other arithmetic: 72.3 us -> 8.06 us
  local copies, waits for them, and re-layouts: 69.1 us -> 8.23 us
  starting transfers between devices: 0.3 us -> 27.6 us
    psum x2 -> x1, waiting for transfers between devices: 1340 us -> 161 us  [body(): dhg = lax.psum(lax.dynamic_update_slice(dhg, top, (n, 0)), 'tp')]
    pallas_call x0 -> x14, Pallas kernels: none -> 569 us  [the longest x3 212 us: rest_rows(): pl.pallas_call(body, out_shape=jax.ShapeDtypeStruct((nb * R, d), jnp.floa...]
    ppermute x0 -> x31, waiting for transfers between devices: none -> 256 us  [hop(): return lambda a: lax.ppermute(a, 'dp', perm)]
    dot_general x3 -> x0, matrix products: 196 us -> none  [the longest x1 66.9 us: local_part(): jnp.einsum('td,vd->tv', h_act, emb_loc, preferred_element_type=jnp.float32)]
    unnamed x17 -> x13, local copies, waits for them, and re-layouts: 68.5 us -> 1.48 us
    reduce_sum x4 -> x5, other arithmetic: 35.6 us -> 3.94 us  [the longest x2 2.06 us: body(): own_loss = jnp.where(tp == 0, jnp.sum(mx + jnp.log(sm)), 0.0) - jnp.sum(hit)]
    ppermute x0 -> x31, starting transfers between devices: none -> 27.6 us  [hop(): return lambda a: lax.ppermute(a, 'dp', perm)]
    convert_element_type x1, other arithmetic: 26.7 us -> 0.7 us  [body(): tgt = jnp.where((tgt >= 0) & (tgt < vocab), tgt, -1).astype(jnp.float32)]
  transfers between devices with their start and end apart: 2 -> 32, of which waited for: 2 -> 7; matrix products, arithmetic and copies ran while one was open for 5% -> 1% of each run, Pallas kernels for 0% -> 49%
where the time goes in v1:
time: 1070 us
  Pallas kernels  569 us (53%)
  waiting for transfers between devices  417 us (39%)
  starting transfers between devices  27.6 us (3%)
  blocking collectives  20.1 us (2%)
  between operations  16.1 us (2%)
    ppermute x31, waiting for transfers between devices, hop(): return lambda a: lax.ppermute(a, 'dp', perm)  256 us
    pallas_call x3, Pallas kernels, rest_rows(): pl.pallas_call(body, out_shape=jax.ShapeDtypeStruct((nb * R, d), jnp.floa...  212 us
    psum x1, waiting for transfers between devices, body(): dhg = lax.psum(lax.dynamic_update_slice(dhg, top, (n, 0)), 'tp')  161 us
    pallas_call x1, Pallas kernels, backward_h(): pl.pallas_call(functools.partial(dh_body, vocab, inv_n), grid=(lg.shape[0...  72.4 us
    pallas_call x2, Pallas kernels, place(): pl.pallas_call(functools.partial(place_body, jobs), out_shape=jax.ShapeDt...  69.4 us
    pallas_call x1, Pallas kernels, forward(): pl.pallas_call(functools.partial(fwd_body, vocab), grid=(nb,), out_shape=...  66.2 us
    pallas_call x2, Pallas kernels, plane_rows(): pl.pallas_call(functools.partial(plane_rows_body, np_, int(own is not Non...  65.1 us
    pallas_call x1, Pallas kernels, chip_rows(): pl.pallas_call(body, out_shape=jax.ShapeDtypeStruct((nb * R, d), jnp.floa...  56.3 us
  transfers between devices with their start and end apart: 32, of which 7 were waited for; matrix products, arithmetic and copies ran while one was open for 1% of the time, Pallas kernels for 49%

profile of v1, /device:TPU:1, one launch (start us, length us, event | category | flops | bytes accessed | tf_op | source)
XLA Modules:
  0.0 1066.2 jit_solution(3501256881378776297)
XLA Ops:
  7.2 6.3 norm_fwd.2
  13.6 6.4 norm_fwd.3
  19.9 2.1 collective-permute-start.7
  25.3 87.2 %collective-permute-done.7.refs_9_ = f32[512,2048]{1,0:T(8,128)} collective-permute-done((f32[512,2048]{1,0:T(8,128)}, f32[512,2048]{1,0:T(8,128)}, u32[]{:S(2)}, u32[]{:S(2)}) %collective-permute-start.7) | collective-permute-done | bytes 4194336 | tf_op jit(solution)/shard_map/ppermute | solution.py:423
  112.6 2.1 collective-permute-start
  114.7 1.7 collective-permute-start.11
  116.4 66.2 %forward.1 = (f32[12800,1024]{1,0:T(8,128)}, f32[8,1024]{1,0:T(8,128)}) custom-call(bf16[1024,2048]{1,0:T(8,128)(2,1)} %get-tuple-element.25.h_ref.refs_1_, bf16[12572,2048]{1,0:T(8,128)(2,1)} %e_ref.15), custom_call_target="tpu_custom_call" | custom-call | flops 52730789888 | bytes 102989824 | tf_op jit(solution)/shard_map/forward/pallas_call | solution.py:103
  183.3 10.7 %all-gather.2 = f32[4,2,1024]{2,1,0:T(2,128)S(1)} all-gather(f32[1,2,1024]{2,1,0:T(2,128)S(1)} %slice_bitcast_fusion.1), channel_id=2, replica_groups=mesh['tp'=4,'dp'=8] {'tp'}, dimensions={0}, use_global_device_ids=true | all-gather | bytes 40960 | tf_op jit(solution)/shard_map/all_gather | solution.py:447
  195.4 1.3 maximum_maximum_fusion.st_ref
  196.7 4.7 collective-permute-start.9
  201.5 1.9 collective-permute-done.2.refs_4_
  203.6 2.9 collective-permute-start.4
  206.7 86.6 %collective-permute-done.11.refs_3_ = f32[512,2048]{1,0:T(8,128)} collective-permute-done((f32[512,2048]{1,0:T(8,128)}, f32[512,2048]{1,0:T(8,128)}, u32[]{:S(2)}, u32[]{:S(2)}) %collective-permute-start.11) | collective-permute-done | bytes 4194336 | tf_op jit(solution)/shard_map/ppermute | solution.py:423
  293.2 1.8 collective-permute-start.8
  295.0 72.4 %backward_h.1 = (f32[1032,2048]{1,0:T(8,128)}, f32[8,1024]{1,0:T(8,128)}) custom-call(f32[12800,1024]{1,0:T(8,128)} %get-tuple-element.26.lg_ref.refs_0_, bf16[12572,2048]{1,0:T(8,128)(2,1)} %e_ref.15, f32[8,1024]{1,0:T(8,128)} %maximum_maximum_fusion.st_ref, f32[1024,1]{1,0:T(8,128)} %get-tuple-element.28.inv_ref, bf16[1024,2048]{1,0:T(8,128)(2,1)} %bitcast.55, ...), custom_call_target="tpu_custom_call" | custom-call | flops 52730789888 | bytes 102989824 | tf_op jit(solution)/shard_map/backward_h/pallas_call | solution.py:166
  367.4 1.5 reduce_sum.48
  372.0 9.4 all-gather.1
  384.5 42.8 %plane_rows.2 = (f32[704,2048]{1,0:T(8,128)}, bf16[7,1024,2048]{2,1,0:T(8,128)(2,1)}) custom-call(s32[6]{0:T(128)} %pad_add_fusion.1.off_ref, bf16[12572,2048]{1,0:T(8,128)(2,1)} %e_ref.15, f32[8,8,1024]{2,1,0:T(8,128)} %copy-done, f32[12800,1024]{1,0:T(8,128)} %get-tuple-element.26.lg_ref.refs_0_, bf16[1024,2048]{1,0:T(8,128)(2,1)} %get-tuple-element.25.h_ref.refs_1_, ...), custom_call_target="tpu_custom_call" | custom-call | flops 29527900160 | bytes 62914560 | tf_op jit(solution)/shard_map/plane_rows/pallas_call | solution.py:269
  427.3 56.3 %chip_rows.1.acc_ref = f32[3520,2048]{1,0:T(8,128)} custom-call(s32[6]{0:T(128)} %pad_add_fusion.1.off_ref, f32[12800,1024]{1,0:T(8,128)} %get-tuple-element.26.lg_ref.refs_0_, bf16[12572,2048]{1,0:T(8,128)(2,1)} %e_ref.15, f32[8,8,1024]{2,1,0:T(8,128)} %copy-done, bf16[1024,2048]{1,0:T(8,128)(2,1)} %get-tuple-element.25.h_ref.refs_1_, ...), custom_call_target="tpu_custom_call" | custom-call | flops 44291850240 | bytes 57671680 | tf_op jit(solution)/shard_map/chip_rows/pallas_call | solution.py:293
  483.6 22.3 %plane_rows.3 = (f32[352,2048]{1,0:T(8,128)}, f32[352,2048]{1,0:T(8,128)}, bf16[7,1024,2048]{2,1,0:T(8,128)(2,1)}) custom-call(s32[6]{0:T(128)} %pad_add_fusion.1.off_ref, bf16[12572,2048]{1,0:T(8,128)(2,1)} %e_ref.15, f32[2,8,1024]{2,1,0:T(8,128)} %slice.54.st_ref, f32[704,2048]{1,0:T(8,128)} %get-tuple-element.35.refs_0_, ...), custom_call_target="tpu_custom_call", output_to_operand_aliasing={{2}: (4, {})} | custom-call | flops 11811160064 | bytes 25165824 | tf_op jit(solution)/shard_map/plane_rows/pallas_call | solution.py:269
  508.7 82.7 %rest_rows.3.refs_3_ = f32[1408,2048]{1,0:T(8,128)} custom-call(s32[6]{0:T(128)} %pad_add_fusion.1.off_ref, bf16[12572,2048]{1,0:T(8,128)(2,1)} %e_ref.15, f32[8,8,1024]{2,1,0:T(8,128)} %copy-done, bf16[7,1024,2048]{2,1,0:T(8,128)(2,1)} %get-tuple-element.36.h_ref, f32[3520,2048]{1,0:T(8,128)} %chip_rows.1.acc_ref), custom_call_target="tpu_custom_call" | custom-call | flops 70866960384 | bytes 28835840 | tf_op jit(solution)/shard_map/rest_rows/pallas_call | solution.py:320
  592.9 82.7 %rest_rows.4.refs_1_ = f32[1408,2048]{1,0:T(8,128)} custom-call(s32[6]{0:T(128)} %pad_add_fusion.1.off_ref, bf16[12572,2048]{1,0:T(8,128)(2,1)} %e_ref.15, f32[8,8,1024]{2,1,0:T(8,128)} %copy-done, bf16[7,1024,2048]{2,1,0:T(8,128)(2,1)} %get-tuple-element.36.h_ref, f32[3520,2048]{1,0:T(8,128)} %chip_rows.1.acc_ref), custom_call_target="tpu_custom_call" | custom-call | flops 70866960384 | bytes 28835840 | tf_op jit(solution)/shard_map/rest_rows/pallas_call | solution.py:320
  680.3 46.6 %rest_rows.5.refs_0_.own_ref = f32[704,2048]{1,0:T(8,128)} custom-call(s32[6]{0:T(128)} %pad_add_fusion.1.off_ref, bf16[12572,2048]{1,0:T(8,128)(2,1)} %e_ref.15, f32[8,8,1024]{2,1,0:T(8,128)} %copy-done, bf16[7,1024,2048]{2,1,0:T(8,128)(2,1)} %get-tuple-element.36.h_ref, f32[3520,2048]{1,0:T(8,128)} %chip_rows.1.acc_ref), custom_call_target="tpu_custom_call" | custom-call | flops 35433480192 | bytes 14417920 | tf_op jit(solution)/shard_map/rest_rows/pallas_call | solution.py:320
  727.0 16.6 %collective-permute-done.19.refs_18_ = f32[352,2048]{1,0:T(8,128)} collective-permute-done((f32[352,2048]{1,0:T(8,128)}, f32[352,2048]{1,0:T(8,128)}, u32[]{:S(2)}, u32[]{:S(2)}) %collective-permute-start.19) | collective-permute-done | bytes 2883616 | tf_op jit(solution)/shard_map/ppermute | solution.py:423
  744.9 5.0 collective-permute-done.26.refs_11_
  750.3 58.7 %collective-permute-done.16.refs_17_ = f32[352,2048]{1,0:T(8,128)} collective-permute-done((f32[352,2048]{1,0:T(8,128)}, f32[352,2048]{1,0:T(8,128)}, u32[]{:S(2)}, u32[]{:S(2)}) %collective-permute-start.16) | collective-permute-done | bytes 2883616 | tf_op jit(solution)/shard_map/ppermute | solution.py:423
  810.7 161.2 %all-reduce.3.cloned.1.call-done.dh_ref = f32[1032,2048]{1,0:T(8,128)} async-done(((f32[1032,2048]{1,0:T(8,128)}), f32[1032,2048]{1,0:T(8,128)}) %all-reduce.3.cloned.1.call-update) | async-done | bytes 8454160 | tf_op jit(solution)/shard_map/psum | solution.py:459
  973.1 1.4 slice.55
  974.5 12.8 %resid_grad.1 = f32[1024,2048]{1,0:T(8,128)} custom-call(f32[1032,2048]{1,0:T(8,128)} %all-reduce.3.cloned.1.call-done.dh_ref, bf16[1024,2048]{1,0:T(8,128)(2,1)} %bitcast.56, f32[1024,2048]{1,0:T(8,128)} %bitcast.52, f32[1024,1]{1,0:T(8,128)} %get-tuple-element.28.inv_ref, f32[1,2048]{1,0:T(1,128)} %bitcast.64), custom_call_target="tpu_custom_call" | custom-call | flops 16777216 | bytes 29360128 | tf_op jit(solution)/shard_map/resid_grad/pallas_call | solution.py:188
  987.3 60.6 %place.2.refs_3_ = f32[12572,2048]{1,0:T(8,128)} custom-call(s32[11]{0:T(128)} %pad_add_fusion.pos_ref, f32[704,2048]{1,0:T(8,128)} %rest_rows.5.refs_0_.own_ref, f32[1408,2048]{1,0:T(8,128)} %rest_rows.4.refs_1_, f32[1408,2048]{1,0:T(8,128)} %collective-permute-done.21.refs_2_, f32[1408,2048]{1,0:T(8,128)} %rest_rows.3.refs_3_, ...), custom_call_target="tpu_custom_call" | custom-call | flops 1000 | bytes 205979648 | tf_op jit(solution)/shard_map/place/pallas_call | solution.py:390
  1048.0 8.7 place.3._
  1056.7 2.2 place_tail.1
  (94 shorter events, 24.4 us)
Async XLA Ops:
  7.2 964.7 %all-reduce.3.cloned.1.call-start = ((), (), s32[]{:S(2)}) async-start(), calls=%async_computation | async-start | bytes 16908288 | tf_op jit(solution)/shard_map/psum | solution.py:459
  19.9 92.6 %collective-permute-start.7 = (f32[512,2048]{1,0:T(8,128)}, f32[512,2048]{1,0:T(8,128)}, u32[]{:S(2)}, u32[]{:S(2)}) collective-permute-start(f32[512,2048]{1,0:T(8,128)} %get-tuple-element.32), channel_id=1, source_target_pairs={{0,4},{1,5},{2,6},{3,7},{4,0},{5,1},{6,2},{7,3},{8,12},{9,13},{10,... | collective-permute-start | bytes 12582920 | tf_op jit(solution)/shard_map/ppermute | solution.py:423
  22.0 92.7 %collective-permute-start.3 = (f32[512,2048]{1,0:T(8,128)}, f32[512,2048]{1,0:T(8,128)}, u32[]{:S(2)}, u32[]{:S(2)}) collective-permute-start(f32[512,2048]{1,0:T(8,128)} %get-tuple-element.32), channel_id=1, source_target_pairs={{0,2},{1,3},{2,0},{3,1},{4,6},{5,7},{6,4},{7,5},{8,10},{9,11},{10,... | collective-permute-start | bytes 12582920 | tf_op jit(solution)/shard_map/ppermute | solution.py:423
  23.2 173.5 %collective-permute-start.1 = (f32[512,2048]{1,0:T(8,128)}, f32[512,2048]{1,0:T(8,128)}, u32[]{:S(2)}, u32[]{:S(2)}) collective-permute-start(f32[512,2048]{1,0:T(8,128)} %get-tuple-element.32), channel_id=1, source_target_pairs={{0,1},{1,0},{2,3},{3,2},{4,5},{5,4},{6,7},{7,6},{8,9},{9,8},{10,11... | collective-permute-start | bytes 12582920 | tf_op jit(solution)/shard_map/ppermute | solution.py:423
  24.4 179.2 %collective-permute-start.6 = (f32[512,2048]{1,0:T(8,128)}, f32[512,2048]{1,0:T(8,128)}, u32[]{:S(2)}, u32[]{:S(2)}) collective-permute-start(f32[512,2048]{1,0:T(8,128)} %get-tuple-element.31), channel_id=1, source_target_pairs={{0,4},{1,5},{2,6},{3,7},{4,0},{5,1},{6,2},{7,3},{8,12},{9,13},{10,... | collective-permute-start | bytes 12582920 | tf_op jit(solution)/shard_map/ppermute | solution.py:423
  24.6 178.7 %collective-permute-start.2 = (f32[512,2048]{1,0:T(8,128)}, f32[512,2048]{1,0:T(8,128)}, u32[]{:S(2)}, u32[]{:S(2)}) collective-permute-start(f32[512,2048]{1,0:T(8,128)} %get-tuple-element.31), channel_id=1, source_target_pairs={{0,2},{1,3},{2,0},{3,1},{4,6},{5,7},{6,4},{7,5},{8,10},{9,11},{10,... | collective-permute-start | bytes 12582920 | tf_op jit(solution)/shard_map/ppermute | solution.py:423
  112.6 94.0 %collective-permute-start = (f32[512,2048]{1,0:T(8,128)}, f32[512,2048]{1,0:T(8,128)}, u32[]{:S(2)}, u32[]{:S(2)}) collective-permute-start(f32[512,2048]{1,0:T(8,128)} %get-tuple-element.31), channel_id=1, source_target_pairs={{0,1},{1,0},{2,3},{3,2},{4,5},{5,4},{6,7},{7,6},{8,9},{9,8},{10,11... | collective-permute-start | bytes 12582920 | tf_op jit(solution)/shard_map/ppermute | solution.py:423
  114.7 178.6 %collective-permute-start.11 = (f32[512,2048]{1,0:T(8,128)}, f32[512,2048]{1,0:T(8,128)}, u32[]{:S(2)}, u32[]{:S(2)}) collective-permute-start(f32[512,2048]{1,0:T(8,128)} %collective-permute-done.7.refs_9_), channel_id=1, source_target_pairs={{0,2},{1,3},{2,0},{3,1},{4,6},{5,7},{6,4},{7,5},{8,10},{9,11},{10,... | collective-permute-start | bytes 12582920 | tf_op jit(solution)/shard_map/ppermute | solution.py:423
  196.7 187.3 %collective-permute-start.9 = (f32[512,2048]{1,0:T(8,128)}, f32[512,2048]{1,0:T(8,128)}, u32[]{:S(2)}, u32[]{:S(2)}) collective-permute-start(f32[512,2048]{1,0:T(8,128)} %collective-permute-done.7.refs_9_), channel_id=1, source_target_pairs={{0,1},{1,0},{2,3},{3,2},{4,5},{5,4},{6,7},{7,6},{8,9},{9,8},{10,11... | collective-permute-start | bytes 12582920 | tf_op jit(solution)/shard_map/ppermute | solution.py:423
  203.3 180.8 %collective-permute-start.10 = (f32[512,2048]{1,0:T(8,128)}, f32[512,2048]{1,0:T(8,128)}, u32[]{:S(2)}, u32[]{:S(2)}) collective-permute-start(f32[512,2048]{1,0:T(8,128)} %collective-permute-done.2.refs_4_), channel_id=1, source_target_pairs={{0,4},{1,5},{2,6},{3,7},{4,0},{5,1},{6,2},{7,3},{8,12},{9,13},{10,... | collective-permute-start | bytes 12582920 | tf_op jit(solution)/shard_map/ppermute | solution.py:423
  203.6 180.9 %collective-permute-start.4 = (f32[512,2048]{1,0:T(8,128)}, f32[512,2048]{1,0:T(8,128)}, u32[]{:S(2)}, u32[]{:S(2)}) collective-permute-start(f32[512,2048]{1,0:T(8,128)} %collective-permute-done.2.refs_4_), channel_id=1, source_target_pairs={{0,1},{1,0},{2,3},{3,2},{4,5},{5,4},{6,7},{7,6},{8,9},{9,8},{10,11... | collective-permute-start | bytes 12582920 | tf_op jit(solution)/shard_map/ppermute | solution.py:423
  206.6 177.9 %collective-permute-start.5 = (f32[512,2048]{1,0:T(8,128)}, f32[512,2048]{1,0:T(8,128)}, u32[]{:S(2)}, u32[]{:S(2)}) collective-permute-start(f32[512,2048]{1,0:T(8,128)} %collective-permute-done.3.refs_5_), channel_id=1, source_target_pairs={{0,1},{1,0},{2,3},{3,2},{4,5},{5,4},{6,7},{7,6},{8,9},{9,8},{10,11... | collective-permute-start | bytes 12582920 | tf_op jit(solution)/shard_map/ppermute | solution.py:423
  293.2 91.3 %collective-permute-start.8 = (f32[512,2048]{1,0:T(8,128)}, f32[512,2048]{1,0:T(8,128)}, u32[]{:S(2)}, u32[]{:S(2)}) collective-permute-start(f32[512,2048]{1,0:T(8,128)} %collective-permute-done.6.refs_8_), channel_id=1, source_target_pairs={{0,1},{1,0},{2,3},{3,2},{4,5},{5,4},{6,7},{7,6},{8,9},{9,8},{10,11... | collective-permute-start | bytes 12582920 | tf_op jit(solution)/shard_map/ppermute | solution.py:423
  384.0 99.6 %collective-permute-start.13 = (f32[512,2048]{1,0:T(8,128)}, f32[512,2048]{1,0:T(8,128)}, u32[]{:S(2)}, u32[]{:S(2)}) collective-permute-start(f32[512,2048]{1,0:T(8,128)} %collective-permute-done.11.refs_3_), channel_id=1, source_target_pairs={{0,1},{1,0},{2,3},{3,2},{4,5},{5,4},{6,7},{7,6},{8,9},{9,8},{10,11... | collective-permute-start | bytes 12582920 | tf_op jit(solution)/shard_map/ppermute | solution.py:423
  384.1 99.5 %collective-permute-start.12 = (f32[512,2048]{1,0:T(8,128)}, f32[512,2048]{1,0:T(8,128)}, u32[]{:S(2)}, u32[]{:S(2)}) collective-permute-start(f32[512,2048]{1,0:T(8,128)} %collective-permute-done.10.refs_2_), channel_id=1, source_target_pairs={{0,1},{1,0},{2,3},{3,2},{4,5},{5,4},{6,7},{7,6},{8,9},{9,8},{10,11... | collective-permute-start | bytes 12582920 | tf_op jit(solution)/shard_map/ppermute | solution.py:423
  505.9 85.5 %collective-permute-start.25 = (f32[352,2048]{1,0:T(8,128)}, f32[352,2048]{1,0:T(8,128)}, u32[]{:S(2)}, u32[]{:S(2)}) collective-permute-start(f32[352,2048]{1,0:T(8,128)} %get-tuple-element.41.refs_6_), channel_id=1, source_target_pairs={{0,2},{1,3},{2,0},{3,1},{4,6},{5,7},{6,4},{7,5},{8,10},{9,11},{10,... | collective-permute-start | bytes 8650760 | tf_op jit(solution)/shard_map/ppermute | solution.py:423
  506.2 86.5 %collective-permute-start.24 = (f32[352,2048]{1,0:T(8,128)}, f32[352,2048]{1,0:T(8,128)}, u32[]{:S(2)}, u32[]{:S(2)}) collective-permute-start(f32[352,2048]{1,0:T(8,128)} %get-tuple-element.41.refs_6_), channel_id=1, source_target_pairs={{0,1},{1,0},{2,3},{3,2},{4,5},{5,4},{6,7},{7,6},{8,9},{9,8},{10,11... | collective-permute-start | bytes 8650760 | tf_op jit(solution)/shard_map/ppermute | solution.py:423
  506.6 169.0 %collective-permute-start.18 = (f32[352,2048]{1,0:T(8,128)}, f32[352,2048]{1,0:T(8,128)}, u32[]{:S(2)}, u32[]{:S(2)}) collective-permute-start(f32[352,2048]{1,0:T(8,128)} %get-tuple-element.41.refs_6_), channel_id=1, source_target_pairs={{0,4},{1,5},{2,6},{3,7},{4,0},{5,1},{6,2},{7,3},{8,12},{9,13},{10,... | collective-permute-start | bytes 8650760 | tf_op jit(solution)/shard_map/ppermute | solution.py:423
  507.8 168.0 %collective-permute-start.28 = (f32[352,2048]{1,0:T(8,128)}, f32[352,2048]{1,0:T(8,128)}, u32[]{:S(2)}, u32[]{:S(2)}) collective-permute-start(f32[352,2048]{1,0:T(8,128)} %get-tuple-element.37.refs_5_), channel_id=1, source_target_pairs={{0,4},{1,5},{2,6},{3,7},{4,0},{5,1},{6,2},{7,3},{8,12},{9,13},{10,... | collective-permute-start | bytes 8650760 | tf_op jit(solution)/shard_map/ppermute | solution.py:423
  508.0 171.1 %collective-permute-start.23 = (f32[352,2048]{1,0:T(8,128)}, f32[352,2048]{1,0:T(8,128)}, u32[]{:S(2)}, u32[]{:S(2)}) collective-permute-start(f32[352,2048]{1,0:T(8,128)} %get-tuple-element.37.refs_5_), channel_id=1, source_target_pairs={{0,1},{1,0},{2,3},{3,2},{4,5},{5,4},{6,7},{7,6},{8,9},{9,8},{10,11... | collective-permute-start | bytes 8650760 | tf_op jit(solution)/shard_map/ppermute | solution.py:423
  591.4 88.1 %collective-permute-start.15 = (f32[352,2048]{1,0:T(8,128)}, f32[352,2048]{1,0:T(8,128)}, u32[]{:S(2)}, u32[]{:S(2)}) collective-permute-start(f32[352,2048]{1,0:T(8,128)} %get-tuple-element.37.refs_5_), channel_id=1, source_target_pairs={{0,2},{1,3},{2,0},{3,1},{4,6},{5,7},{6,4},{7,5},{8,10},{9,11},{10,... | collective-permute-start | bytes 8650760 | tf_op jit(solution)/shard_map/ppermute | solution.py:423
  592.6 87.1 %collective-permute-start.27 = (f32[352,2048]{1,0:T(8,128)}, f32[352,2048]{1,0:T(8,128)}, u32[]{:S(2)}, u32[]{:S(2)}) collective-permute-start(f32[352,2048]{1,0:T(8,128)} %collective-permute-done.25.refs_10_), channel_id=1, source_target_pairs={{0,1},{1,0},{2,3},{3,2},{4,5},{5,4},{6,7},{7,6},{8,9},{9,8},{10,11... | collective-permute-start | bytes 8650760 | tf_op jit(solution)/shard_map/ppermute | solution.py:423
  675.6 311.7 %collective-permute-start.21 = (f32[1408,2048]{1,0:T(8,128)}, f32[1408,2048]{1,0:T(8,128)}, u32[]{:S(2)}, u32[]{:S(2)}) collective-permute-start(f32[1408,2048]{1,0:T(8,128)} %rest_rows.4.refs_1_), channel_id=1, source_target_pairs={{0,1},{1,0},{2,3},{3,2},{4,5},{5,4},{6,7},{7,6},{8,9},{9,8},{10,11... | collective-permute-start | bytes 34603016 | tf_op jit(solution)/shard_map/ppermute | solution.py:423
  675.8 311.4 %collective-permute-start.22 = (f32[1408,2048]{1,0:T(8,128)}, f32[1408,2048]{1,0:T(8,128)}, u32[]{:S(2)}, u32[]{:S(2)}) collective-permute-start(f32[1408,2048]{1,0:T(8,128)} %rest_rows.3.refs_3_), channel_id=1, source_target_pairs={{0,1},{1,0},{2,3},{3,2},{4,5},{5,4},{6,7},{7,6},{8,9},{9,8},{10,11... | collective-permute-start | bytes 34603016 | tf_op jit(solution)/shard_map/ppermute | solution.py:423
  679.2 47.7 %collective-permute-start.30 = (f32[352,2048]{1,0:T(8,128)}, f32[352,2048]{1,0:T(8,128)}, u32[]{:S(2)}, u32[]{:S(2)}) collective-permute-start(f32[352,2048]{1,0:T(8,128)} %collective-permute-done.18.refs_14_), channel_id=1, source_target_pairs={{0,1},{1,0},{2,3},{3,2},{4,5},{5,4},{6,7},{7,6},{8,9},{9,8},{10,11... | collective-permute-start | bytes 8650760 | tf_op jit(solution)/shard_map/ppermute | solution.py:423
  679.5 64.1 %collective-permute-start.19 = (f32[352,2048]{1,0:T(8,128)}, f32[352,2048]{1,0:T(8,128)}, u32[]{:S(2)}, u32[]{:S(2)}) collective-permute-start(f32[352,2048]{1,0:T(8,128)} %collective-permute-done.18.refs_14_), channel_id=1, source_target_pairs={{0,2},{1,3},{2,0},{3,1},{4,6},{5,7},{6,4},{7,5},{8,10},{9,11},{10,... | collective-permute-start | bytes 8650760 | tf_op jit(solution)/shard_map/ppermute | solution.py:423
  679.7 65.0 %collective-permute-start.29 = (f32[352,2048]{1,0:T(8,128)}, f32[352,2048]{1,0:T(8,128)}, u32[]{:S(2)}, u32[]{:S(2)}) collective-permute-start(f32[352,2048]{1,0:T(8,128)} %collective-permute-done.28.refs_13_), channel_id=1, source_target_pairs={{0,1},{1,0},{2,3},{3,2},{4,5},{5,4},{6,7},{7,6},{8,9},{9,8},{10,11... | collective-permute-start | bytes 8650760 | tf_op jit(solution)/shard_map/ppermute | solution.py:423
  726.9 321.1 %collective-permute-start.14 = (f32[704,2048]{1,0:T(8,128)}, f32[704,2048]{1,0:T(8,128)}, u32[]{:S(2)}, u32[]{:S(2)}) collective-permute-start(f32[704,2048]{1,0:T(8,128)} %rest_rows.5.refs_0_.own_ref), channel_id=1, source_target_pairs={{0,1},{1,0},{2,3},{3,2},{4,5},{5,4},{6,7},{7,6},{8,9},{9,8},{10,11... | collective-permute-start | bytes 17301512 | tf_op jit(solution)/shard_map/ppermute | solution.py:423
  743.6 6.4 collective-permute-start.26
  744.7 64.4 %collective-permute-start.16 = (f32[352,2048]{1,0:T(8,128)}, f32[352,2048]{1,0:T(8,128)}, u32[]{:S(2)}, u32[]{:S(2)}) collective-permute-start(f32[352,2048]{1,0:T(8,128)} %collective-permute-done.15.refs_9_), channel_id=1, source_target_pairs={{0,4},{1,5},{2,6},{3,7},{4,0},{5,1},{6,2},{7,3},{8,12},{9,13},{10,... | collective-permute-start | bytes 8650760 | tf_op jit(solution)/shard_map/ppermute | solution.py:423
  750.0 298.0 %collective-permute-start.20 = (f32[352,2048]{1,0:T(8,128)}, f32[352,2048]{1,0:T(8,128)}, u32[]{:S(2)}, u32[]{:S(2)}) collective-permute-start(f32[352,2048]{1,0:T(8,128)} %collective-permute-done.19.refs_18_), channel_id=1, source_target_pairs={{0,1},{1,0},{2,3},{3,2},{4,5},{5,4},{6,7},{7,6},{8,9},{9,8},{10,11... | collective-permute-start | bytes 8650760 | tf_op jit(solution)/shard_map/ppermute | solution.py:423
  809.1 238.9 %collective-permute-start.17 = (f32[352,2048]{1,0:T(8,128)}, f32[352,2048]{1,0:T(8,128)}, u32[]{:S(2)}, u32[]{:S(2)}) collective-permute-start(f32[352,2048]{1,0:T(8,128)} %collective-permute-done.16.refs_17_), channel_id=1, source_target_pairs={{0,1},{1,0},{2,3},{3,2},{4,5},{5,4},{6,7},{7,6},{8,9},{9,8},{10,11... | collective-permute-start | bytes 8650760 | tf_op jit(solution)/shard_map/ppermute | solution.py:423
  (5 other events, 7.3 us)
Sparse Core Ops, SparseCore 0:
  679.3 292.5 all-reduce.2

commit v2 on v1

--- a/solution.py
+++ b/solution.py
@@ -17,9 +17,10 @@
 VB = 1280
 SUB = 256
 TB = 128
-R = 704
+RA = 864
+R = 576
 NF = 5
-GROUPS = (2, 2, 1)
+GROUPS = (3, 2)
 
 
 def params(**kw):
@@ -110,7 +111,7 @@
         compiler_params=params(), name="forward")(h, emb)
 
 
-def dh_body(vocab, inv_n, lg_ref, e_ref, st_ref, inv_ref, hid_ref, res_ref, dh_ref, t_ref, hid_scr, res_scr, t_scr, sem):
+def dh_body(vocab, inv_n, lg_ref, e_ref, st_ref, inv_ref, hid_ref, res_ref, dh_ref, hid_scr, res_scr, t_scr, sem):
     i = pl.program_id(0)
     n = st_ref.shape[1]
     loads = [pltpu.make_async_copy(hid_ref, hid_scr, sem.at[0]), pltpu.make_async_copy(res_ref, res_scr, sem.at[1])]
@@ -149,8 +150,12 @@
     def _():
         for c in loads:
             c.wait()
-        t_ref[...] = t_scr[...]
-        acc = jnp.zeros((8, dh_ref.shape[1]), jnp.float32)
+        d = dh_ref.shape[1]
+        once = (lax.broadcasted_iota(jnp.int32, (8, 1), 0) == 0) & (lax.axis_index('tp') == 0)
+        lse = st_ref[0:1] + jnp.log(st_ref[3:4])
+        dh_ref[pl.ds(n + 8, 8), pl.ds(0, n)] = jnp.where(once, lse, 0.0) - t_scr[...]
+        dh_ref[pl.ds(n + 8, 8), pl.ds(n, d - n)] = jnp.zeros((8, d - n), jnp.float32)
+        acc = jnp.zeros((8, d), jnp.float32)
         for q in range(n // TB):
             rows = pl.ds(q * TB, TB)
             v = dh_ref[rows, :] * ((res_scr[rows, :] + hid_scr[rows, :].astype(jnp.float32)) * inv_ref[rows, :])
@@ -165,10 +170,10 @@
     any_space = pl.BlockSpec(memory_space=pl.ANY)
     return pl.pallas_call(
         functools.partial(dh_body, vocab, inv_n), grid=(lg.shape[0] // VB,),
-        out_shape=(jax.ShapeDtypeStruct((n + 8, d), jnp.float32), jax.ShapeDtypeStruct((8, n), jnp.float32)),
+        out_shape=jax.ShapeDtypeStruct((n + 16, d), jnp.float32),
         in_specs=[pl.BlockSpec((VB, n), lambda i: (i, 0)), pl.BlockSpec((VB, d), lambda i: (i, 0)), whole((8, n)), whole((n, 1)),
                   any_space, any_space],
-        out_specs=[whole((n + 8, d)), pl.BlockSpec((8, n), lambda i: (0, 0))],
+        out_specs=whole((n + 16, d)),
         scratch_shapes=[pltpu.VMEM((n, d), jnp.bfloat16), pltpu.VMEM((n, d), jnp.float32), pltpu.VMEM((8, n), jnp.float32),
                         pltpu.SemaphoreType.DMA((2,))],
         cost_estimate=cost(2 * n * d * vocab, 2 * vocab * d + 4 * n * vocab, n * vocab),
@@ -191,6 +196,54 @@
         cost_estimate=cost(8 * n * d, 14 * n * d), compiler_params=params(), name="resid_grad")(dh, hid, res, inv, w)
 
 
+MESH = pl.DeviceIdType.MESH
+
+
+HOPS = ("", "c", "x", "y", "xc", "yc", "xy", "xyc")
+
+
+def flipped(dp, hop):
+    c, x, y = dp % 2, dp // 2 % 2, dp // 4
+    x, y, c = [1 - v if name in hop else v for name, v in zip("xyc", (x, y, c))]
+    return y * 4 + x * 2 + c
+
+
+def meet(peers):
+    barrier = pltpu.get_barrier_semaphore()
+    for p in peers:
+        pl.semaphore_signal(barrier, inc=1, device_id=p, device_id_type=MESH)
+    pl.semaphore_wait(barrier, len(peers))
+
+
+def stats_body(n_tp, vocab, inv_n, st_ref, tgt_ref, out_ref, got, send, recv):
+    tp = lax.axis_index('tp')
+    peers = [{'tp': (tp + k) % n_tp} for k in range(1, n_tp)]
+    meet(peers)
+    copies = [pltpu.make_async_remote_copy(src_ref=st_ref, dst_ref=got.at[k], send_sem=send.at[k], recv_sem=recv.at[k],
+                                           device_id=p, device_id_type=MESH) for k, p in enumerate(peers)]
+    for c in copies:
+        c.start()
+    for c in copies:
+        c.wait()
+    st = [st_ref[...]] + [got[k] for k in range(len(peers))]
+    mx = functools.reduce(jnp.maximum, [v[0:1] for v in st])
+    sm = sum(v[1:2] * jnp.exp(v[0:1] - mx) for v in st)
+    t = tgt_ref[...] - (tp * vocab).astype(jnp.float32)
+    t = jnp.where((t >= 0) & (t < vocab), t, -1.0)
+    row = lax.broadcasted_iota(jnp.int32, (8, 1), 0)
+    out_ref[...] = jnp.where(row == 0, mx, jnp.where(row == 1, inv_n / sm, jnp.where(row == 2, t, sm)))
+
+
+def exchange_stats(st, tgt, n_tp, vocab, inv_n):
+    n = st.shape[1]
+    vm = pl.BlockSpec(memory_space=pltpu.VMEM)
+    return pl.pallas_call(
+        functools.partial(stats_body, n_tp, vocab, inv_n), out_shape=jax.ShapeDtypeStruct((8, n), jnp.float32),
+        in_specs=[vm, vm], out_specs=vm,
+        scratch_shapes=[pltpu.VMEM((n_tp - 1, 8, n), jnp.float32)] + [pltpu.SemaphoreType.DMA((n_tp - 1,))] * 2,
+        compiler_params=pltpu.CompilerParams(collective_id=0, has_side_effects=True), name="exchange_stats")(st, tgt)
+
+
 def dlogits(l, st, base, inv_n):
     row = lax.broadcasted_iota(jnp.int32, (l.shape[0], 1), 0).astype(jnp.float32)
     p = jnp.exp(l - st[0:1]) * st[1:2]
@@ -205,33 +258,57 @@
     return lax.dot_general(a, b, NN, preferred_element_type=jnp.float32)
 
 
-def plane_rows_body(np_, own, split, inv_n, off_ref, e_ref, st_ref, *refs):
+def plane_rows_body(nl, ns, own, split, inv_n, e_ref, st_ref, *refs):
     if own:
         lg_ref, hb_ref, refs = refs[0], refs[1], refs[2:]
     else:
         acc_ref, refs = refs[0], refs[2:]
-    h_refs, refs = refs[:2 * np_], refs[2 * np_:]
+    h_refs, refs = refs[:2 * nl], refs[2 * nl:]
     out_refs, refs = refs[:split], refs[split:]
-    all_ref, buf, h_scr, sem = refs
+    all_ref, refs = refs[0], refs[1:]
+    if own:
+        land, refs = refs[0], refs[1:]
+    buf, h_scr, sem, send, recv = refs
     i = pl.program_id(0)
     half = buf.shape[1] // 2
+    dp = lax.axis_index('dp')
+    other = {'dp': flipped(dp, "c")}
 
     def load(k, slot):
-        return [pltpu.make_async_copy(h_refs[2 * k + u], buf.at[slot, pl.ds(u * half, half)], sem.at[slot, u]) for u in range(2)]
+        cs = []
+        for u in range(2):
+            src = h_refs[2 * k + u] if k < nl else land.at[k - nl, pl.ds(u * half, half)]
+            cs.append(pltpu.make_async_copy(src, buf.at[slot, pl.ds(u * half, half)], sem.at[slot, u]))
+        return cs
+
+    def over(k):
+        cs = []
+        for u in range(2):
+            dst = land.at[k, pl.ds(u * half, half)] if own else buf.at[1, pl.ds(u * half, half)]
+            cs.append(pltpu.make_async_remote_copy(src_ref=h_refs[2 * (nl - ns + k) + u], dst_ref=dst, send_sem=send.at[k, u],
+                                                   recv_sem=recv.at[k, u], device_id=other, device_id_type=MESH))
+        return cs
 
     @pl.when(i == 0)
     def _():
         for c in load(0, 0):
             c.start()
-
-    for k in range(1, np_):
+        meet([other])
+        for k in range(ns):
+            for c in over(k):
+                c.start()
+
+    for k in range(1, nl + ns if own else nl):
         @pl.when(i + 1 == k)
         def _():
+            if k >= nl:
+                for c in over(k - nl):
+                    c.wait_recv()
             for c in load(k, k % 2):
                 c.start()
 
-    base = off_ref[0].astype(jnp.float32)
-    rh = R // 2
+    base = (dp * RA).astype(jnp.float32)
+    rh = RA // 2
 
     @pl.when(i == 0)
     def _():
@@ -243,8 +320,19 @@
                 o[pl.ds(at, rh), :] = acc_ref[pl.ds(u * rh, rh), :]
 
     slot = lax.rem(i, 2)
-    for u in range(2):
-        pltpu.make_async_copy(h_refs[u], buf.at[slot, pl.ds(u * half, half)], sem.at[slot, u]).wait()
+    if own:
+        for u in range(2):
+            pltpu.make_async_copy(h_refs[u], buf.at[slot, pl.ds(u * half, half)], sem.at[slot, u]).wait()
+    else:
+        @pl.when(i == 0)
+        def _():
+            for c in load(0, 0):
+                c.wait()
+
+        @pl.when(i == 1)
+        def _():
+            for c in over(0):
+                c.wait_recv()
     h_scr[...] = buf[slot].astype(jnp.bfloat16)
     all_ref[...] = h_scr[...]
 
@@ -254,42 +342,51 @@
         o, at = out_refs[u % split], 0 if split == 2 else u * rh
         o[pl.ds(at, rh), :] += nn(dlogits(ls[u], st, base + u * rh, inv_n), h_scr[...])
 
-
-def plane_rows(off, emb, st, parts, inv_n, split, slots, own=None, acc=None, so_far=None):
-    np_, (half, d) = len(parts) // 2, parts[0].shape
-    n = 2 * half
+    @pl.when(i == nl + ns - 1)
+    def _():
+        for k in range(ns):
+            for c in over(k):
+                c.wait_send()
+
+
+def plane_rows(emb, st, parts, ns, inv_n, split, slots, own=None, acc=None, so_far=None):
+    nl, (half, d) = len(parts) // 2, parts[0].shape
+    n, np_ = 2 * half, nl + ns
     one = pl.Buffered(1)
-    at = lambda i, off: (pl.multiple_of(off[0], 16), 0)
-    whole_r = lambda r: pl.BlockSpec((r, d), lambda i, off: (0, 0), pipeline_mode=one)
+    at = lambda i: (lax.axis_index('dp'), 0)
+    whole_r = lambda r: pl.BlockSpec((r, d), lambda i: (0, 0), pipeline_mode=one)
     any_space = pl.BlockSpec(memory_space=pl.ANY)
+    out_shape = [jax.ShapeDtypeStruct((RA // split, d), jnp.float32)] * split + [jax.ShapeDtypeStruct((7, n, d), jnp.bfloat16)]
+    out_specs = [whole_r(RA // split)] * split + [pl.BlockSpec((None, n, d), lambda i: (slots(i), 0, 0))]
     if own is not None:
-        lead, specs = list(own), [pl.BlockSpec((pl.Element(R), pl.Element(n)), at, pipeline_mode=one), whole((n, d))]
+        lead, specs = list(own), [pl.BlockSpec((RA, n), at, pipeline_mode=one), whole((n, d))]
+        out_shape.append(jax.ShapeDtypeStruct((ns, n, d), jnp.float32))
+        out_specs.append(any_space)
     else:
-        lead, specs = [acc, so_far], [whole_r(R), any_space]
-    return pl.pallas_call(
-        functools.partial(plane_rows_body, np_, int(own is not None), split, inv_n),
-        out_shape=tuple([jax.ShapeDtypeStruct((R // split, d), jnp.float32)] * split + [jax.ShapeDtypeStruct((7, n, d), jnp.bfloat16)]),
-        grid_spec=pltpu.PrefetchScalarGridSpec(
-            num_scalar_prefetch=1, grid=(np_,),
-            in_specs=[pl.BlockSpec((pl.Element(R, (0, R)), pl.Element(d)), at, pipeline_mode=one), whole(st.shape)] + specs
-            + [any_space] * (2 * np_),
-            out_specs=tuple([whole_r(R // split)] * split + [pl.BlockSpec((None, n, d), lambda i, off: (slots(i), 0, 0))]),
-            scratch_shapes=[pltpu.VMEM((2, n, d), jnp.float32), pltpu.VMEM((n, d), jnp.bfloat16), pltpu.SemaphoreType.DMA((2, 2))]),
-        input_output_aliases={} if own is not None else {4: split},
-        cost_estimate=cost(4 * np_ * n * d * R, 6 * np_ * n * d, np_ * n * R),
-        compiler_params=params(), name="plane_rows")(off, emb, st, *lead, *parts)
+        lead, specs = [acc, so_far], [whole_r(RA), any_space]
+    out = pl.pallas_call(
+        functools.partial(plane_rows_body, nl, ns, int(own is not None), split, inv_n), grid=(np_,), out_shape=tuple(out_shape),
+        in_specs=[pl.BlockSpec((RA, d), at, pipeline_mode=one),
+                  whole((8, 8, n)) if own is not None else pl.BlockSpec((2, 8, n), lambda i: (3, 0, 0), pipeline_mode=one)] + specs + [any_space] * (2 * nl),
+        out_specs=tuple(out_specs),
+        scratch_shapes=[pltpu.VMEM((2, n, d), jnp.float32), pltpu.VMEM((n, d), jnp.bfloat16), pltpu.SemaphoreType.DMA((2, 2)),
+                        pltpu.SemaphoreType.DMA((ns, 2)), pltpu.SemaphoreType.DMA((ns, 2))],
+        input_output_aliases={} if own is not None else {3: split},
+        cost_estimate=cost(4 * np_ * n * d * RA, 6 * np_ * n * d, np_ * n * RA),
+        compiler_params=params(collective_id=2 + (own is None), has_side_effects=True), name="plane_rows")(emb, st, *lead, *parts)
+    return out[:split + 1]
 
 
 def chip_rows(off, lg, emb, st, hb, hs, slot, nb, inv_n):
     n, d = hb.shape
 
     def body(off_ref, lg_ref, e_ref, st_ref, h_ref, s_ref, out_ref):
-        base = off_ref[1 + pl.program_id(0)].astype(jnp.float32)
+        base = off_ref[pl.program_id(0)].astype(jnp.float32)
         l = nt(e_ref[...], s_ref[...])
         out_ref[...] = nn(dlogits(lg_ref[...], st_ref[0], base, inv_n), h_ref[...])
         out_ref[...] += nn(dlogits(l, st_ref[1], base, inv_n), s_ref[...])
 
-    at = lambda i, off: (pl.multiple_of(off[1 + i], 16), 0)
+    at = lambda i, off: (pl.multiple_of(off[i], 16), 0)
     return pl.pallas_call(
         body, out_shape=jax.ShapeDtypeStruct((nb * R, d), jnp.float32),
         grid_spec=pltpu.PrefetchScalarGridSpec(
@@ -301,36 +398,77 @@
         compiler_params=params(), name="chip_rows")(off, lg, emb, st, hb, hs)
 
 
-def rest_rows(off, b0, nb, ng, emb, st, acc, hs, inv_n):
+def rest_rows(off, b0, nb, ng, emb, st, acc, hs, inv_n, out):
     n, d = hs.shape[1], hs.shape[2]
-
-    def body(off_ref, e_ref, st_ref, h_ref, acc_ref, out_ref):
+    vocab = emb.shape[0]
+    ends = b0 + nb == NF
+    short = (vocab - 8 * RA - (2 * NF - 1) * R) // 8 * 8
+
+    def body(off_ref, e_ref, st_ref, h_ref, acc_ref, *refs):
+        f_ref, out_ref, sem = refs[-3:]
         i, j = pl.program_id(0), pl.program_id(1)
-        base = off_ref[1 + b0 + i].astype(jnp.float32)
+        row0 = off_ref[b0 + i]
+        base = row0.astype(jnp.float32)
         l = nt(e_ref[...], h_ref[0])
         for q in range(2):
             after = nt(e_ref[...], h_ref[1]) if q == 0 else None
             x = nn(dlogits(l, st_ref[q], base, inv_n), h_ref[q])
             if q == 0:
-                out_ref[...] = jnp.where(j == 0, acc_ref[...], out_ref[...]) + x
+                f_ref[...] = jnp.where(j == 0, acc_ref[...], f_ref[...]) + x
             else:
-                out_ref[...] += x
+                f_ref[...] += x
             l = after
 
-    return pl.pallas_call(
-        body, out_shape=jax.ShapeDtypeStruct((nb * R, d), jnp.float32),
+        def put(rows, at=row0):
+            return pltpu.make_async_copy(f_ref.at[pl.ds(0, rows)], out_ref.at[pl.ds(pl.multiple_of(at, 8), rows)], sem)
+
+        @pl.when(j == ng - 1)
+        def _():
+            @pl.when(i > 0)
+            def _():
+                put(R, off_ref[b0 + i - 1]).wait()
+
+            @pl.when(i < nb - 1)
+            def _():
+                put(R).start()
+
+            @pl.when(i == nb - 1)
+            def _():
+                if ends:
+                    past = row0 + R > vocab
+
+                    @pl.when(past)
+                    def _():
+                        put(short).start()
+                        put(short).wait()
+
+                    @pl.when(jnp.logical_not(past))
+                    def _():
+                        put(R).start()
+                        put(R).wait()
+                else:
+                    put(R).start()
+                    put(R).wait()
+
+    any_space = pl.BlockSpec(memory_space=pl.ANY)
+    ops = [emb, st, hs, acc] + ([] if out is None else [out])
+    return pl.pallas_call(
+        body, out_shape=(jax.ShapeDtypeStruct((nb * R, d), jnp.float32), jax.ShapeDtypeStruct((vocab, d), jnp.float32)),
         grid_spec=pltpu.PrefetchScalarGridSpec(
             num_scalar_prefetch=1, grid=(nb, ng),
-            in_specs=[pl.BlockSpec((pl.Element(R, (0, R)), pl.Element(d)), lambda i, j, off: (pl.multiple_of(off[1 + b0 + i], 16), 0)),
+            in_specs=[pl.BlockSpec((pl.Element(R, (0, R)), pl.Element(d)), lambda i, j, off: (pl.multiple_of(off[b0 + i], 16), 0)),
                       pl.BlockSpec((2, 8, n), lambda i, j, off: (j + 1, 0, 0)), pl.BlockSpec((2, n, d), lambda i, j, off: (j, 0, 0)),
-                      pl.BlockSpec((R, d), lambda i, j, off: (b0 + i, 0))],
-            out_specs=pl.BlockSpec((R, d), lambda i, j, off: (i, 0))),
+                      pl.BlockSpec((R, d), lambda i, j, off: (b0 + i, 0))] + [any_space] * (out is not None),
+            out_specs=(pl.BlockSpec((R, d), lambda i, j, off: (i, 0)), any_space),
+            scratch_shapes=[pltpu.SemaphoreType.DMA]),
+        input_output_aliases={} if out is None else {5: 1},
         cost_estimate=cost(4 * 2 * ng * n * d * nb * R, 10 * d * nb * R, 2 * ng * n * nb * R),
-        compiler_params=params(), name="rest_rows")(off, emb, st, hs, acc)
+        compiler_params=params(), name="rest_rows")(off, *ops)
 
 
 NBUF = 8
-CH = 200
+CH = 216
+LAST = 10
 
 
 def place_body(jobs, pos_ref, *refs):
@@ -379,11 +517,11 @@
 
 def place(pos, pieces, vocab, d, tail, so_far=None):
     jobs, ops = [], []
-    for arr, k, add, ends in pieces:
+    for arr, k, add in pieces:
         ops.append(arr)
         for r0 in range(0, arr.shape[0], CH):
             rows = min(CH, arr.shape[0] - r0)
-            short = max(0, min(rows, (tail - add - r0) // 8 * 8)) if ends else rows
+            short = max(0, min(rows, (tail - add - r0) // 8 * 8)) if k == LAST else rows
             jobs.append((len(ops) - 1, r0, rows, k, add + r0, short))
     if so_far is not None:
         ops.append(so_far)
@@ -413,16 +551,12 @@
 
 
 def solution(mesh):
-    n_dp = mesh.shape['dp']
-
-    def hop(dx, dy, dc):
-        perm = []
-        for i in range(n_dp):
-            c, x, y = i % 2, (i // 2) % 2, i // 4
-            perm.append((i, ((y ^ dy) * 2 + (x ^ dx)) * 2 + (c ^ dc)))
-        return lambda a: lax.ppermute(a, 'dp', perm)
-
-    over_x, over_y, over_c = hop(1, 0, 0), hop(0, 1, 0), hop(0, 0, 1)
+    n_dp, n_tp = mesh.shape['dp'], mesh.shape['tp']
+
+    def over(hop, a):
+        return lax.ppermute(a, 'dp', [(i, flipped(i, hop)) for i in range(n_dp)])
+
+    over_x, over_y, over_c = [functools.partial(over, hop) for hop in "xyc"]
 
     def program(hidden, residual, targets, embedding, norm_w):
         n_tok = hidden.shape[0] * hidden.shape[1]
@@ -433,43 +567,36 @@
             hid, res = hid_loc.reshape(n, d), res_loc.reshape(n, d)
             vocab = emb.shape[0]
             w = norm_vec.reshape(1, d)
-            tp, dp = lax.axis_index('tp'), lax.axis_index('dp')
+            dp = lax.axis_index('dp')
             hb, inv, hf1 = norm_fwd(hid, res, w, 0)
             x1 = over_x(hf1)
             hb, inv, hf2 = norm_fwd(hid, res, w, 1, (hb, inv))
             y2 = over_y(hf2)
-            x2, y1, s1, s2 = over_x(hf2), over_y(hf1), over_c(hf1), over_c(hf2)
+            x2, y1 = over_x(hf2), over_y(hf1)
+            s1, s2 = over_c(hf1), over_c(hf2)
             d1, d2 = over_y(x1), over_x(y2)
-            xs1, ys2 = over_c(x1), over_c(y2)
-            xs2, ys1 = over_c(x2), over_c(y1)
-            ds1, ds2 = over_c(d1), over_c(d2)
             lg, st = forward(hb, emb)
-            st = lax.all_gather(st[0:2], 'tp', axis=0)
-            mx = jnp.max(st[:, 0], axis=0)
-            sm = jnp.sum(st[:, 1] * jnp.exp(st[:, 0] - mx), axis=0)
-            tgt = tgt_loc.reshape(n) - tp * vocab
-            tgt = jnp.where((tgt >= 0) & (tgt < vocab), tgt, -1).astype(jnp.float32)
-            mine = jnp.concatenate([jnp.stack([mx, inv_n / sm, tgt]), jnp.zeros((5, n), jnp.float32)], axis=0)
-            dhg, hit = backward_h(lg, emb, mine, inv, hid, res, inv_n)
-            own_loss = jnp.where(tp == 0, jnp.sum(mx + jnp.log(sm)), 0.0) - jnp.sum(hit)
-            extra = jnp.concatenate([jnp.sum(dhg[n:], axis=0), jnp.full((n,), own_loss * inv_n)]).reshape(3, n)
-            plane = lax.all_gather(jnp.concatenate([mine[0:3], extra, mine[6:8]], axis=0), 'dp', axis=0)
-            sums = jnp.sum(plane[:, 3:6], axis=0).reshape(3 * n)
-            top = jnp.concatenate([jnp.stack([sums[:d], jnp.broadcast_to(sums[2 * n], (d,))]), jnp.zeros((6, d), jnp.float32)], axis=0)
-            dhg = lax.psum(lax.dynamic_update_slice(dhg, top, (n, 0)), 'tp')
-            grad_w, loss = dhg[n], dhg[n + 1, 0]
-            order = jnp.stack([dp ^ k for k in range(n_dp)])
-            plane = plane[order]
-
-            f0 = n_dp * R
+            mine = exchange_stats(st, tgt_loc.reshape(1, n).astype(jnp.float32), n_tp, vocab, inv_n)
+            plane = jnp.stack([mine] + [over(hop, mine) for hop in HOPS[1:]])
+            dhg = backward_h(lg, emb, mine, inv, hid, res, inv_n)
+            dhg = lax.psum(dhg, 'tp')
+            sums = jnp.concatenate([jnp.sum(dhg[n:n + 8], axis=0), jnp.full((n,), jnp.sum(dhg[n + 8:]) * inv_n)]).reshape(3 * n // 128, 128)
+            for hop in "cxy":
+                back = over(hop, sums)
+                sums = sums + back
+            sums = sums.reshape(3 * n)
+            grad_w, loss = sums[:d], sums[2 * n]
+            order = jnp.stack([flipped(dp, hop) for hop in HOPS])
+
+            f0 = n_dp * RA
             fh = NF * R
             core = dp % 2
-            off = jnp.concatenate([jnp.stack([dp * R]), f0 + core * fh + R * jnp.arange(NF)]).astype(jnp.int32)
+            off = (f0 + core * fh + R * jnp.arange(NF)).astype(jnp.int32)
             gate = lax.optimization_barrier
-            a, hs = plane_rows(off, emb, plane, [s1, s2, x1, x2, xs1, xs2, y1, y2, ys1, ys2], inv_n, 1, lambda i: lax.rem(i + 6, 7), own=(lg, hb))
+            a, hs = plane_rows(emb, plane, [s1, s2, x1, x2, y1, y2], 2, inv_n, 1, lambda i: lax.rem(i + 6, 7), own=(lg, hb))
             acc = chip_rows(off, lg, emb, plane, hb, hs, 6, NF, inv_n)
             a, _ = gate((a, acc))
-            a1, a2, hs = plane_rows(off, emb, plane[6:8], [d1, d2, ds1, ds2], inv_n, 2, lambda i: i + 4, acc=a, so_far=hs)
+            a1, a2, hs = plane_rows(emb, plane, [d1, d2], 1, inv_n, 2, lambda i: i + 4, acc=a, so_far=hs)
             ax1, ay2 = over_x(a1), over_y(a2)
             ax2, ay1 = over_x(a2), over_y(a1)
             as1, as2 = over_c(a1), over_c(a2)
@@ -478,24 +605,31 @@
             axs2, ays1 = over_c(ax2), over_c(ay1)
             ads1, ads2 = over_c(ad1), over_c(ad2)
             pieces, last, j = [], a1, 0
-            for k, (p1, p2) in enumerate([(a1, a2), (as1, as2), (ax1, ax2), (axs1, axs2), (ay1, ay2), (ays1, ays2), (ad1, ad2), (ads1, ads2)]):
-                pieces += [(p1, 1 + k, 0, False), (p2, 1 + k, R // 2, False)]
+            for k, (p1, p2) in enumerate([(a1, a2), (as1, as2), (ax1, ax2), (ay1, ay2), (axs1, axs2), (ays1, ays2), (ad1, ad2), (ads1, ads2)]):
+                pieces += [(p1, 1 + k, 0), (p2, 1 + k, RA // 2)]
             tail = vocab - f0 - fh
+            grad_emb = None
             for cnt in GROUPS:
                 acc, last = gate((acc, last))
-                last = rest_rows(off, j, cnt, 3, emb, plane, acc, hs, inv_n)
+                last, grad_emb = rest_rows(off, j, cnt, 3, emb, plane, acc, hs, inv_n, grad_emb)
                 other = over_c(last)
-                pieces = [(last, 9, j * R, True), (other, 10, j * R, True)] + pieces
+                pieces = [(other, LAST, j * R)] + pieces
                 if j * R <= tail < (j + cnt) * R:
                     ending = (last, other, tail // 8 * 8 - j * R)
                 j += cnt
-            pos = jnp.concatenate([jnp.stack([f0 + fh]), order * R, jnp.stack([f0 + core * fh, f0 + (1 - core) * fh])]).astype(jnp.int32)
-            late = [p for p in pieces if p[0] is ads1 or p[0] is ads2 or p[0] is other]
-            grad_emb = place(pos, [p for p in pieces if all(p[0] is not q[0] for q in late)], vocab, d, tail)
-            grad_emb = place(pos, late, vocab, d, tail, grad_emb)
+            pos = jnp.concatenate([jnp.stack([f0 + fh]), order * RA, jnp.stack([f0 + core * fh, f0 + (1 - core) * fh])]).astype(jnp.int32)
+
+            def of(*arrays):
+                return [p for p in pieces if any(p[0] is q for q in arrays)]
+
+            early = [p for p in pieces if all(p[0] is not q for q in (axs2, ays1, ad1, ad2, ads1, ads2, other))]
+            grad_emb = place(pos, early, vocab, d, tail, grad_emb)
+            grad_r = resid_grad(dhg, hid, res, inv, w)
+            grad_emb, grad_r = gate((grad_emb, grad_r))
+            grad_emb = place(pos, of(other, axs2, ays1, ad1, ad2), vocab, d, tail, grad_emb)
+            grad_emb = place(pos, of(ads1, ads2), vocab, d, tail, grad_emb)
             if vocab % 8:
                 grad_emb = place_tail(pos, *ending, grad_emb)
-            grad_r = resid_grad(dhg, hid, res, inv, w)
             return loss, grad_r.reshape(hid_loc.shape), grad_emb, grad_w
 
         sharded = jax.shard_map(

time: 1070 us -> 879 us (0.82)
  waiting for transfers between devices: 417 us -> 267 us
  Pallas kernels: 569 us -> 539 us
  blocking collectives: 20.1 us -> 0 us
    psum x1, waiting for transfers between devices: 161 us -> 0.02 us  [body(): dhg = lax.psum(dhg, 'tp')]
    all_gather x2 -> x0, blocking collectives: 20.1 us -> none  [the longest x1 10.7 us: body(): st = lax.all_gather(st[0:2], 'tp', axis=0)]
    pallas_call x2 -> x3, Pallas kernels: 69.4 us -> 57.4 us  [place(): pl.pallas_call(functools.partial(place_body, jobs), out_shape=jax.ShapeDt...]
    ppermute x31 -> x34, waiting for transfers between devices: 256 us -> 267 us  [over(): return lax.ppermute(a, 'dp', [(i, flipped(i, hop)) for i in range(n_dp)])]
    ppermute x31 -> x34, starting transfers between devices: 27.6 us -> 33.1 us  [over(): return lax.ppermute(a, 'dp', [(i, flipped(i, hop)) for i in range(n_dp)])]
  transfers between devices with their start and end apart: 32 -> 35, of which waited for: 7 -> 10; matrix products, arithmetic and copies ran while one was open for 1% -> 2% of each run, Pallas kernels for 49% -> 60%
where the time goes in v2:
time: 879 us; the launch traced here: 872 us
  Pallas kernels  539 us (61%)
  waiting for transfers between devices  267 us (30%)
  starting transfers between devices  33.2 us (4%)
  between operations  15.1 us (2%)
  local copies, waits for them, and re-layouts  12.7 us (1%)
    ppermute x34, waiting for transfers between devices, over(): return lax.ppermute(a, 'dp', [(i, flipped(i, hop)) for i in range(n_dp)])  267 us
    pallas_call x2, Pallas kernels, rest_rows(): pl.pallas_call(body, out_shape=(jax.ShapeDtypeStruct((nb * R, d), jnp.flo...  173 us
    pallas_call x2, Pallas kernels, plane_rows(): pl.pallas_call(functools.partial(plane_rows_body, nl, ns, int(own is not...  85.5 us
    pallas_call x1, Pallas kernels, backward_h(): pl.pallas_call(functools.partial(dh_body, vocab, inv_n), grid=(lg.shape[0...  72.4 us
    pallas_call x1, Pallas kernels, forward(): pl.pallas_call(functools.partial(fwd_body, vocab), grid=(nb,), out_shape=...  66.1 us
    pallas_call x3, Pallas kernels, place(): pl.pallas_call(functools.partial(place_body, jobs), out_shape=jax.ShapeDt...  57.4 us
    pallas_call x1, Pallas kernels, chip_rows(): pl.pallas_call(body, out_shape=jax.ShapeDtypeStruct((nb * R, d), jnp.floa...  47.3 us
    ppermute x34, starting transfers between devices, over(): return lax.ppermute(a, 'dp', [(i, flipped(i, hop)) for i in range(n_dp)])  33.1 us
  transfers between devices with their start and end apart: 35, of which 10 were waited for; matrix products, arithmetic and copies ran while one was open for 2% of the time, Pallas kernels for 60%

profile of v2, /device:TPU:1, one launch (start us, length us, event | category | flops | bytes accessed | tf_op | source)
XLA Modules:
  0.0 871.6 jit_solution(14090947988065370797)
XLA Ops:
  7.2 6.4 norm_fwd.2
  14.9 6.4 norm_fwd.3
  21.3 66.1 %forward.1 = (f32[12800,1024]{1,0:T(8,128)}, f32[8,1024]{1,0:T(8,128)}) custom-call(bf16[1024,2048]{1,0:T(8,128)(2,1)} %get-tuple-element.28.h_ref.refs_1_, bf16[12572,2048]{1,0:T(8,128)(2,1)} %e_ref.13), custom_call_target="tpu_custom_call" | custom-call | flops 52730789888 | bytes 102989824 | tf_op jit(solution)/shard_map/forward/pallas_call | solution.py:104
  87.4 9.7 %exchange_stats.1.st_ref = f32[8,1024]{1,0:T(8,128)} custom-call(f32[8,1024]{1,0:T(8,128)} %get-tuple-element.30.st_ref, f32[1,1024]{1,0:T(1,128)} %convert_element_type.3.tgt_ref), custom_call_target="tpu_custom_call" | custom-call | tf_op jit(solution)/shard_map/exchange_stats/pallas_call | solution.py:240
  100.9 2.2 collective-permute-start.8
  103.1 1.5 collective-permute-start.9
  104.6 1.6 collective-permute-start.12
  109.1 72.4 %backward_h.1 = f32[1040,2048]{1,0:T(8,128)} custom-call(f32[12800,1024]{1,0:T(8,128)} %get-tuple-element.29.lg_ref.refs_0_, bf16[12572,2048]{1,0:T(8,128)(2,1)} %e_ref.13, f32[8,1024]{1,0:T(8,128)} %exchange_stats.1.st_ref, f32[1024,1]{1,0:T(8,128)} %get-tuple-element.31.inv_ref, bf16[1024,2048]{1,0:T(8,128)(2,1)} %bitcast.46, f32[1024,2048]{1,0:T(8,128)} %bitcast.42), custom_call_target="tpu_custom_call" | custom-call | flops 52730789888 | bytes 102989824 | tf_op jit(solution)/shard_map/backward_h/pallas_call | solution.py:171
  192.4 5.3 collective-permute-done.12.refs_4_
  199.1 89.1 %collective-permute-done.15.refs_7_ = f32[512,2048]{1,0:T(8,128)} collective-permute-done((f32[512,2048]{1,0:T(8,128)}, f32[512,2048]{1,0:T(8,128)}, u32[]{:S(2)}, u32[]{:S(2)}) %collective-permute-start.15) | collective-permute-done | bytes 4194336 | tf_op jit(solution)/shard_map/ppermute | solution.py:557
  289.3 55.4 %plane_rows.2 = (f32[864,2048]{1,0:T(8,128)}, bf16[7,1024,2048]{2,1,0:T(8,128)(2,1)}, f32[2,1024,2048]{2,1,0:T(8,128)}) custom-call(bf16[12572,2048]{1,0:T(8,128)(2,1)} %e_ref.13, f32[8,8,1024]{2,1,0:T(8,128)} %bitcast_dynamic-update-slice_fusion.st_ref, f32[12800,1024]{1,0:T(8,128)} %get-tuple-element.29.lg_ref.refs_0_, ...), custom_call_target="tpu_custom_call" | custom-call | flops 36238786560 | bytes 62914560 | tf_op jit(solution)/shard_map/plane_rows/pallas_call | solution.py:367
  344.7 47.3 %chip_rows.1.acc_ref = f32[2880,2048]{1,0:T(8,128)} custom-call(s32[5]{0:T(128)} %multiply_add_fusion.off_ref, f32[12800,1024]{1,0:T(8,128)} %get-tuple-element.29.lg_ref.refs_0_, bf16[12572,2048]{1,0:T(8,128)(2,1)} %e_ref.13, f32[8,8,1024]{2,1,0:T(8,128)} %bitcast_dynamic-update-slice_fusion.st_ref, bf16[1024,2048]{1,0:T(8,128)(2,1)} %get-tuple-element.28.h_ref.refs_1_, ...), custom_call_target="tpu_custom_call" | custom-call | flops 36238786560 | bytes 47185920 | tf_op jit(solution)/shard_map/chip_rows/pallas_call | solution.py:390
  391.9 30.1 %plane_rows.3 = (f32[432,2048]{1,0:T(8,128)}, f32[432,2048]{1,0:T(8,128)}, bf16[7,1024,2048]{2,1,0:T(8,128)(2,1)}) custom-call(bf16[12572,2048]{1,0:T(8,128)(2,1)} %e_ref.13, f32[8,8,1024]{2,1,0:T(8,128)} %bitcast_dynamic-update-slice_fusion.st_ref, f32[864,2048]{1,0:T(8,128)} %get-tuple-element.36.refs_0_, ...), custom_call_target="tpu_custom_call", output_to_operand_aliasing={{2}: (3, {})} | custom-call | flops 14495514624 | bytes 25165824 | tf_op jit(solution)/shard_map/plane_rows/pallas_call | solution.py:367
  422.2 1.6 collective-permute-start.21
  424.4 101.7 %rest_rows.2 = (f32[1728,2048]{1,0:T(8,128)}, f32[12572,2048]{1,0:T(8,128)}) custom-call(s32[5]{0:T(128)} %multiply_add_fusion.off_ref, bf16[12572,2048]{1,0:T(8,128)(2,1)} %e_ref.13, f32[8,8,1024]{2,1,0:T(8,128)} %bitcast_dynamic-update-slice_fusion.st_ref, bf16[7,1024,2048]{2,1,0:T(8,128)(2,1)} %get-tuple-element.37.h_ref, f32[2880,2048]{1,0:T(8,128)} %chip_rows.1.acc_ref), custom_call_target="tpu_custom_call" | custom-call | flops 86973087744 | bytes 35389440 | tf_op jit(solution)/shard_map/rest_rows/pallas_call | solution.py:455
  526.2 1.5 slice_reduce_fusion
  528.9 19.0 %collective-permute-done = f32[24,128]{1,0:T(8,128)S(1)} collective-permute-done((f32[24,128]{1,0:T(8,128)S(1)}, f32[24,128]{1,0:T(8,128)S(1)}, u32[]{:S(2)}, u32[]{:S(2)}) %collective-permute-start) | collective-permute-done | bytes 12320 | tf_op jit(solution)/shard_map/ppermute | solution.py:557
  547.9 2.5 collective-permute-done.1
  552.0 1.6 collective-permute-done.2
  555.7 3.2 collective-permute-start.25
  558.9 71.0 %rest_rows.3 = (f32[1152,2048]{1,0:T(8,128)}, f32[12572,2048]{1,0:T(8,128)}) custom-call(s32[5]{0:T(128)} %multiply_add_fusion.off_ref, bf16[12572,2048]{1,0:T(8,128)(2,1)} %e_ref.13, f32[8,8,1024]{2,1,0:T(8,128)} %bitcast_dynamic-update-slice_fusion.st_ref, bf16[7,1024,2048]{2,1,0:T(8,128)(2,1)} %get-tuple-element.37.h_ref, ...), custom_call_target="tpu_custom_call", output_to_operand_aliasing={{1}: (5, {})} | custom-call | flops 57982058496 | bytes 23592960 | tf_op jit(solution)/shard_map/rest_rows/pallas_call | solution.py:455
  630.2 3.3 collective-permute-start.27
  633.5 72.3 %collective-permute-done.24.refs_8_ = f32[432,2048]{1,0:T(8,128)} collective-permute-done((f32[432,2048]{1,0:T(8,128)}, f32[432,2048]{1,0:T(8,128)}, u32[]{:S(2)}, u32[]{:S(2)}) %collective-permute-start.24) | collective-permute-done | bytes 3538976 | tf_op jit(solution)/shard_map/ppermute | solution.py:557
  705.8 3.5 collective-permute-start.26
  710.2 1.5 collective-permute-start.30
  711.7 3.8 collective-permute-done.26.refs_10_
  715.9 71.8 %collective-permute-done.28.refs_3_ = f32[432,2048]{1,0:T(8,128)} collective-permute-done((f32[432,2048]{1,0:T(8,128)}, f32[432,2048]{1,0:T(8,128)}, u32[]{:S(2)}, u32[]{:S(2)}) %collective-permute-start.28) | collective-permute-done | bytes 3538976 | tf_op jit(solution)/shard_map/ppermute | solution.py:557
  790.3 12.7 %resid_grad.1 = f32[1024,2048]{1,0:T(8,128)} custom-call(f32[1040,2048]{1,0:T(8,128)} %all-reduce.3.cloned.1.call-done.dh_ref, bf16[1024,2048]{1,0:T(8,128)(2,1)} %bitcast.47, f32[1024,2048]{1,0:T(8,128)} %bitcast.43, f32[1024,1]{1,0:T(8,128)} %get-tuple-element.31.inv_ref, f32[1,2048]{1,0:T(1,128)} %bitcast.51), custom_call_target="tpu_custom_call" | custom-call | flops 16777216 | bytes 29360128 | tf_op jit(solution)/shard_map/resid_grad/pallas_call | solution.py:193
  804.8 33.8 %place.3.refs_5_ = f32[12572,2048]{1,0:T(8,128)} custom-call(s32[11]{0:T(128)} %pad_add_fusion.pos_ref, f32[1728,2048]{1,0:T(8,128)} %collective-permute-done.18.refs_0_, f32[432,2048]{1,0:T(8,128)} %get-tuple-element.38.refs_1_, f32[432,2048]{1,0:T(8,128)} %get-tuple-element.41.refs_2_, ...), custom_call_target="tpu_custom_call", output_to_operand_aliasing={{}: (12, {})} | custom-call | flops 1000 | bytes 205979648 | tf_op jit(solution)/shard_map/place/pallas_call | solution.py:528
  838.7 17.1 %place.4.refs_2_ = f32[12572,2048]{1,0:T(8,128)} custom-call(s32[11]{0:T(128)} %pad_add_fusion.pos_ref, f32[1152,2048]{1,0:T(8,128)} %collective-permute-done.27.refs_0_.other_ref, f32[432,2048]{1,0:T(8,128)} %collective-permute-done.32.refs_1_, f32[432,2048]{1,0:T(8,128)} %collective-permute-done.33.refs_2_, ...), custom_call_target="tpu_custom_call", output_to_operand_aliasing={{}: (6, {})} | custom-call | flops 1000 | bytes 205979648 | tf_op jit(solution)/shard_map/place/pallas_call | solution.py:528
  855.8 6.6 place.5._
  862.4 2.2 place_tail.1
  (80 shorter events, 32.3 us)
Async XLA Ops:
  7.2 519.0 %all-reduce.3.cloned.1.call-start = ((), (), s32[]{:S(2)}) async-start(), calls=%async_computation | async-start | bytes 17039360 | tf_op jit(solution)/shard_map/psum | solution.py:582
  13.6 94.5 %collective-permute-start.10 = (f32[512,2048]{1,0:T(8,128)}, f32[512,2048]{1,0:T(8,128)}, u32[]{:S(2)}, u32[]{:S(2)}) collective-permute-start(f32[512,2048]{1,0:T(8,128)} %get-tuple-element.32), channel_id=1, source_target_pairs={{0,1},{1,0},{2,3},{3,2},{4,5},{5,4},{6,7},{7,6},{8,9},{9,8},{10,11... | collective-permute-start | bytes 12582920 | tf_op jit(solution)/shard_map/ppermute | solution.py:557
  97.1 3.8 collective-permute-start.3
  98.9 4.2 collective-permute-start.5
  100.2 4.4 collective-permute-start.6
  100.9 5.2 collective-permute-start.7
  100.9 5.2 collective-permute-start.8
  103.1 4.6 collective-permute-start.9
  104.6 93.2 %collective-permute-start.12 = (f32[512,2048]{1,0:T(8,128)}, f32[512,2048]{1,0:T(8,128)}, u32[]{:S(2)}, u32[]{:S(2)}) collective-permute-start(f32[512,2048]{1,0:T(8,128)} %get-tuple-element.32), channel_id=1, source_target_pairs={{0,2},{1,3},{2,0},{3,1},{4,6},{5,7},{6,4},{7,5},{8,10},{9,11},{10,... | collective-permute-start | bytes 12582920 | tf_op jit(solution)/shard_map/ppermute | solution.py:557
  106.2 183.1 %collective-permute-start.11 = (f32[512,2048]{1,0:T(8,128)}, f32[512,2048]{1,0:T(8,128)}, u32[]{:S(2)}, u32[]{:S(2)}) collective-permute-start(f32[512,2048]{1,0:T(8,128)} %get-tuple-element.33), channel_id=1, source_target_pairs={{0,1},{1,0},{2,3},{3,2},{4,5},{5,4},{6,7},{7,6},{8,9},{9,8},{10,11... | collective-permute-start | bytes 12582920 | tf_op jit(solution)/shard_map/ppermute | solution.py:557
  106.2 183.1 %collective-permute-start.13 = (f32[512,2048]{1,0:T(8,128)}, f32[512,2048]{1,0:T(8,128)}, u32[]{:S(2)}, u32[]{:S(2)}) collective-permute-start(f32[512,2048]{1,0:T(8,128)} %get-tuple-element.33), channel_id=1, source_target_pairs={{0,2},{1,3},{2,0},{3,1},{4,6},{5,7},{6,4},{7,5},{8,10},{9,11},{10,... | collective-permute-start | bytes 12582920 | tf_op jit(solution)/shard_map/ppermute | solution.py:557
  107.7 181.6 %collective-permute-start.14 = (f32[512,2048]{1,0:T(8,128)}, f32[512,2048]{1,0:T(8,128)}, u32[]{:S(2)}, u32[]{:S(2)}) collective-permute-start(f32[512,2048]{1,0:T(8,128)} %get-tuple-element.32), channel_id=1, source_target_pairs={{0,4},{1,5},{2,6},{3,7},{4,0},{5,1},{6,2},{7,3},{8,12},{9,13},{10,... | collective-permute-start | bytes 12582920 | tf_op jit(solution)/shard_map/ppermute | solution.py:557
  108.0 180.2 %collective-permute-start.15 = (f32[512,2048]{1,0:T(8,128)}, f32[512,2048]{1,0:T(8,128)}, u32[]{:S(2)}, u32[]{:S(2)}) collective-permute-start(f32[512,2048]{1,0:T(8,128)} %get-tuple-element.33), channel_id=1, source_target_pairs={{0,4},{1,5},{2,6},{3,7},{4,0},{5,1},{6,2},{7,3},{8,12},{9,13},{10,... | collective-permute-start | bytes 12582920 | tf_op jit(solution)/shard_map/ppermute | solution.py:557
  197.8 194.2 %collective-permute-start.16 = (f32[512,2048]{1,0:T(8,128)}, f32[512,2048]{1,0:T(8,128)}, u32[]{:S(2)}, u32[]{:S(2)}) collective-permute-start(f32[512,2048]{1,0:T(8,128)} %collective-permute-done.12.refs_4_), channel_id=1, source_target_pairs={{0,4},{1,5},{2,6},{3,7},{4,0},{5,1},{6,2},{7,3},{8,12},{9,13},{10,... | collective-permute-start | bytes 12582920 | tf_op jit(solution)/shard_map/ppermute | solution.py:557
  288.3 103.6 %collective-permute-start.17 = (f32[512,2048]{1,0:T(8,128)}, f32[512,2048]{1,0:T(8,128)}, u32[]{:S(2)}, u32[]{:S(2)}) collective-permute-start(f32[512,2048]{1,0:T(8,128)} %collective-permute-done.15.refs_7_), channel_id=1, source_target_pairs={{0,2},{1,3},{2,0},{3,1},{4,6},{5,7},{6,4},{7,5},{8,10},{9,11},{10,... | collective-permute-start | bytes 12582920 | tf_op jit(solution)/shard_map/ppermute | solution.py:557
  422.1 132.1 %collective-permute-start.19 = (f32[432,2048]{1,0:T(8,128)}, f32[432,2048]{1,0:T(8,128)}, u32[]{:S(2)}, u32[]{:S(2)}) collective-permute-start(f32[432,2048]{1,0:T(8,128)} %get-tuple-element.38.refs_1_), channel_id=1, source_target_pairs={{0,1},{1,0},{2,3},{3,2},{4,5},{5,4},{6,7},{7,6},{8,9},{9,8},{10,11... | collective-permute-start | bytes 10616840 | tf_op jit(solution)/shard_map/ppermute | solution.py:557
  422.2 133.5 %collective-permute-start.21 = (f32[432,2048]{1,0:T(8,128)}, f32[432,2048]{1,0:T(8,128)}, u32[]{:S(2)}, u32[]{:S(2)}) collective-permute-start(f32[432,2048]{1,0:T(8,128)} %get-tuple-element.38.refs_1_), channel_id=1, source_target_pairs={{0,2},{1,3},{2,0},{3,1},{4,6},{5,7},{6,4},{7,5},{8,10},{9,11},{10,... | collective-permute-start | bytes 10616840 | tf_op jit(solution)/shard_map/ppermute | solution.py:557
  423.7 131.4 %collective-permute-start.20 = (f32[432,2048]{1,0:T(8,128)}, f32[432,2048]{1,0:T(8,128)}, u32[]{:S(2)}, u32[]{:S(2)}) collective-permute-start(f32[432,2048]{1,0:T(8,128)} %get-tuple-element.41.refs_2_), channel_id=1, source_target_pairs={{0,1},{1,0},{2,3},{3,2},{4,5},{5,4},{6,7},{7,6},{8,9},{9,8},{10,11... | collective-permute-start | bytes 10616840 | tf_op jit(solution)/shard_map/ppermute | solution.py:557
  526.1 263.4 %collective-permute-start.18 = (f32[1728,2048]{1,0:T(8,128)}, f32[1728,2048]{1,0:T(8,128)}, u32[]{:S(2)}, u32[]{:S(2)}) collective-permute-start(f32[1728,2048]{1,0:T(8,128)} %get-tuple-element.40), channel_id=1, source_target_pairs={{0,1},{1,0},{2,3},{3,2},{4,5},{5,4},{6,7},{7,6},{8,9},{9,8},{10,11... | collective-permute-start | bytes 42467336 | tf_op jit(solution)/shard_map/ppermute | solution.py:557
  528.4 19.5 %collective-permute-start = (f32[24,128]{1,0:T(8,128)S(1)}, f32[24,128]{1,0:T(8,128)S(1)}, u32[]{:S(2)}, u32[]{:S(2)}) collective-permute-start(f32[24,128]{1,0:T(8,128)S(1)} %pad_bitcast_fusion), channel_id=1, source_target_pairs={{0,1},{1,0},{2,3},{3,2},{4,5},{5,4},{6,7},{7,6},{8,9},{9,8},{10,11... | collective-permute-start | bytes 36872 | tf_op jit(solution)/shard_map/ppermute | solution.py:557
  554.2 76.0 %collective-permute-start.22 = (f32[432,2048]{1,0:T(8,128)}, f32[432,2048]{1,0:T(8,128)}, u32[]{:S(2)}, u32[]{:S(2)}) collective-permute-start(f32[432,2048]{1,0:T(8,128)} %get-tuple-element.41.refs_2_), channel_id=1, source_target_pairs={{0,2},{1,3},{2,0},{3,1},{4,6},{5,7},{6,4},{7,5},{8,10},{9,11},{10,... | collective-permute-start | bytes 10616840 | tf_op jit(solution)/shard_map/ppermute | solution.py:557
  554.2 155.1 %collective-permute-start.23 = (f32[432,2048]{1,0:T(8,128)}, f32[432,2048]{1,0:T(8,128)}, u32[]{:S(2)}, u32[]{:S(2)}) collective-permute-start(f32[432,2048]{1,0:T(8,128)} %get-tuple-element.38.refs_1_), channel_id=1, source_target_pairs={{0,4},{1,5},{2,6},{3,7},{4,0},{5,1},{6,2},{7,3},{8,12},{9,13},{10,... | collective-permute-start | bytes 10616840 | tf_op jit(solution)/shard_map/ppermute | solution.py:557
  555.1 150.6 %collective-permute-start.24 = (f32[432,2048]{1,0:T(8,128)}, f32[432,2048]{1,0:T(8,128)}, u32[]{:S(2)}, u32[]{:S(2)}) collective-permute-start(f32[432,2048]{1,0:T(8,128)} %get-tuple-element.41.refs_2_), channel_id=1, source_target_pairs={{0,4},{1,5},{2,6},{3,7},{4,0},{5,1},{6,2},{7,3},{8,12},{9,13},{10,... | collective-permute-start | bytes 10616840 | tf_op jit(solution)/shard_map/ppermute | solution.py:557
  555.7 154.6 %collective-permute-start.25 = (f32[432,2048]{1,0:T(8,128)}, f32[432,2048]{1,0:T(8,128)}, u32[]{:S(2)}, u32[]{:S(2)}) collective-permute-start(f32[432,2048]{1,0:T(8,128)} %collective-permute-done.21.refs_5_), channel_id=1, source_target_pairs={{0,1},{1,0},{2,3},{3,2},{4,5},{5,4},{6,7},{7,6},{8,9},{9,8},{10,11... | collective-permute-start | bytes 10616840 | tf_op jit(solution)/shard_map/ppermute | solution.py:557
  630.2 208.5 %collective-permute-start.27 = (f32[1152,2048]{1,0:T(8,128)}, f32[1152,2048]{1,0:T(8,128)}, u32[]{:S(2)}, u32[]{:S(2)}) collective-permute-start(f32[1152,2048]{1,0:T(8,128)} %get-tuple-element.46.own_ref), channel_id=1, source_target_pairs={{0,1},{1,0},{2,3},{3,2},{4,5},{5,4},{6,7},{7,6},{8,9},{9,8},{10,11... | collective-permute-start | bytes 28311560 | tf_op jit(solution)/shard_map/ppermute | solution.py:557
  705.8 9.7 %collective-permute-start.26 = (f32[432,2048]{1,0:T(8,128)}, f32[432,2048]{1,0:T(8,128)}, u32[]{:S(2)}, u32[]{:S(2)}) collective-permute-start(f32[432,2048]{1,0:T(8,128)} %collective-permute-done.24.refs_8_), channel_id=1, source_target_pairs={{0,1},{1,0},{2,3},{3,2},{4,5},{5,4},{6,7},{7,6},{8,9},{9,8},{10,11... | collective-permute-start | bytes 10616840 | tf_op jit(solution)/shard_map/ppermute | solution.py:557
  709.3 78.4 %collective-permute-start.28 = (f32[432,2048]{1,0:T(8,128)}, f32[432,2048]{1,0:T(8,128)}, u32[]{:S(2)}, u32[]{:S(2)}) collective-permute-start(f32[432,2048]{1,0:T(8,128)} %collective-permute-done.21.refs_5_), channel_id=1, source_target_pairs={{0,4},{1,5},{2,6},{3,7},{4,0},{5,1},{6,2},{7,3},{8,12},{9,13},{10,... | collective-permute-start | bytes 10616840 | tf_op jit(solution)/shard_map/ppermute | solution.py:557
  710.2 78.3 %collective-permute-start.30 = (f32[432,2048]{1,0:T(8,128)}, f32[432,2048]{1,0:T(8,128)}, u32[]{:S(2)}, u32[]{:S(2)}) collective-permute-start(f32[432,2048]{1,0:T(8,128)} %collective-permute-done.24.refs_8_), channel_id=1, source_target_pairs={{0,2},{1,3},{2,0},{3,1},{4,6},{5,7},{6,4},{7,5},{8,10},{9,11},{10,... | collective-permute-start | bytes 10616840 | tf_op jit(solution)/shard_map/ppermute | solution.py:557
  715.5 123.2 %collective-permute-start.32 = (f32[432,2048]{1,0:T(8,128)}, f32[432,2048]{1,0:T(8,128)}, u32[]{:S(2)}, u32[]{:S(2)}) collective-permute-start(f32[432,2048]{1,0:T(8,128)} %collective-permute-done.22.refs_6_), channel_id=1, source_target_pairs={{0,1},{1,0},{2,3},{3,2},{4,5},{5,4},{6,7},{7,6},{8,9},{9,8},{10,11... | collective-permute-start | bytes 10616840 | tf_op jit(solution)/shard_map/ppermute | solution.py:557
  787.7 51.0 %collective-permute-start.33 = (f32[432,2048]{1,0:T(8,128)}, f32[432,2048]{1,0:T(8,128)}, u32[]{:S(2)}, u32[]{:S(2)}) collective-permute-start(f32[432,2048]{1,0:T(8,128)} %collective-permute-done.23.refs_7_), channel_id=1, source_target_pairs={{0,1},{1,0},{2,3},{3,2},{4,5},{5,4},{6,7},{7,6},{8,9},{9,8},{10,11... | collective-permute-start | bytes 10616840 | tf_op jit(solution)/shard_map/ppermute | solution.py:557
  788.6 67.2 %collective-permute-start.29 = (f32[432,2048]{1,0:T(8,128)}, f32[432,2048]{1,0:T(8,128)}, u32[]{:S(2)}, u32[]{:S(2)}) collective-permute-start(f32[432,2048]{1,0:T(8,128)} %collective-permute-done.28.refs_3_), channel_id=1, source_target_pairs={{0,1},{1,0},{2,3},{3,2},{4,5},{5,4},{6,7},{7,6},{8,9},{9,8},{10,11... | collective-permute-start | bytes 10616840 | tf_op jit(solution)/shard_map/ppermute | solution.py:557
  789.5 66.3 %collective-permute-start.31 = (f32[432,2048]{1,0:T(8,128)}, f32[432,2048]{1,0:T(8,128)}, u32[]{:S(2)}, u32[]{:S(2)}) collective-permute-start(f32[432,2048]{1,0:T(8,128)} %collective-permute-done.30.refs_4_), channel_id=1, source_target_pairs={{0,1},{1,0},{2,3},{3,2},{4,5},{5,4},{6,7},{7,6},{8,9},{9,8},{10,11... | collective-permute-start | bytes 10616840 | tf_op jit(solution)/shard_map/ppermute | solution.py:557
  (6 other events, 10.3 us)
Sparse Core Ops, SparseCore 0:
  181.7 296.1 all-reduce.2

commit v3 on v2

--- a/solution.py
+++ b/solution.py
@@ -17,8 +17,8 @@
 VB = 1280
 SUB = 256
 TB = 128
-RA = 864
-R = 576
+RA = 896
+R = 544
 NF = 5
 GROUPS = (3, 2)
 
@@ -467,7 +467,7 @@
 
 
 NBUF = 8
-CH = 216
+CH = 224
 LAST = 10
 
 
@@ -626,7 +626,8 @@
             grad_emb = place(pos, early, vocab, d, tail, grad_emb)
             grad_r = resid_grad(dhg, hid, res, inv, w)
             grad_emb, grad_r = gate((grad_emb, grad_r))
-            grad_emb = place(pos, of(other, axs2, ays1, ad1, ad2), vocab, d, tail, grad_emb)
+            grad_emb = place(pos, of(other, axs2, ays1), vocab, d, tail, grad_emb)
+            grad_emb = place(pos, of(ad1, ad2), vocab, d, tail, grad_emb)
             grad_emb = place(pos, of(ads1, ads2), vocab, d, tail, grad_emb)
             if vocab % 8:
                 grad_emb = place_tail(pos, *ending, grad_emb)

time: 879 us -> 885 us (level)
  waiting for transfers between devices: 267 us -> 278 us
    ppermute x34, waiting for transfers between devices: 267 us -> 278 us  [over(): return lax.ppermute(a, 'dp', [(i, flipped(i, hop)) for i in range(n_dp)])]
    pallas_call x3 -> x4, Pallas kernels: 57.4 us -> 60.1 us  [place(): pl.pallas_call(functools.partial(place_body, jobs), out_shape=jax.ShapeDt...]
  transfers between devices with their start and end apart: 35 -> 35, of which waited for: 10 -> 10; matrix products, arithmetic and copies ran while one was open for 2% -> 2% of each run, Pallas kernels for 60% -> 59%
where the time goes in v3:
time: 885 us; the launch traced here: 877 us
  Pallas kernels  532 us (60%)
  waiting for transfers between devices  278 us (31%)
  starting transfers between devices  32.9 us (4%)
  between operations  15.3 us (2%)
  local copies, waits for them, and re-layouts  14 us (2%)
    ppermute x34, waiting for transfers between devices, over(): return lax.ppermute(a, 'dp', [(i, flipped(i, hop)) for i in range(n_dp)])  278 us
    pallas_call x2, Pallas kernels, rest_rows(): pl.pallas_call(body, out_shape=(jax.ShapeDtypeStruct((nb * R, d), jnp.flo...  164 us
    pallas_call x2, Pallas kernels, plane_rows(): pl.pallas_call(functools.partial(plane_rows_body, nl, ns, int(own is not...  87.4 us
    pallas_call x1, Pallas kernels, backward_h(): pl.pallas_call(functools.partial(dh_body, vocab, inv_n), grid=(lg.shape[0...  72.4 us
    pallas_call x1, Pallas kernels, forward(): pl.pallas_call(functools.partial(fwd_body, vocab), grid=(nb,), out_shape=...  66.2 us
    pallas_call x4, Pallas kernels, place(): pl.pallas_call(functools.partial(place_body, jobs), out_shape=jax.ShapeDt...  60.1 us
    pallas_call x1, Pallas kernels, chip_rows(): pl.pallas_call(body, out_shape=jax.ShapeDtypeStruct((nb * R, d), jnp.floa...  44.9 us
    ppermute x34, starting transfers between devices, over(): return lax.ppermute(a, 'dp', [(i, flipped(i, hop)) for i in range(n_dp)])  32.9 us
  transfers between devices with their start and end apart: 35, of which 10 were waited for; matrix products, arithmetic and copies ran while one was open for 2% of the time, Pallas kernels for 59%

profile of v3, /device:TPU:1, one launch (start us, length us, event | category | flops | bytes accessed | tf_op | source)
XLA Modules:
  0.0 877.3 jit_solution(6735023566006771834)
XLA Ops:
  7.2 6.4 norm_fwd.2
  14.9 6.4 norm_fwd.3
  21.3 66.2 %forward.1 = (f32[12800,1024]{1,0:T(8,128)}, f32[8,1024]{1,0:T(8,128)}) custom-call(bf16[1024,2048]{1,0:T(8,128)(2,1)} %get-tuple-element.28.h_ref.refs_1_, bf16[12572,2048]{1,0:T(8,128)(2,1)} %e_ref.13), custom_call_target="tpu_custom_call" | custom-call | flops 52730789888 | bytes 102989824 | tf_op jit(solution)/shard_map/forward/pallas_call | solution.py:104
  87.4 9.7 %exchange_stats.1.st_ref = f32[8,1024]{1,0:T(8,128)} custom-call(f32[8,1024]{1,0:T(8,128)} %get-tuple-element.30.st_ref, f32[1,1024]{1,0:T(1,128)} %convert_element_type.3.tgt_ref), custom_call_target="tpu_custom_call" | custom-call | tf_op jit(solution)/shard_map/exchange_stats/pallas_call | solution.py:240
  101.0 2.2 collective-permute-start.8
  103.1 1.5 collective-permute-start.9
  104.6 1.6 collective-permute-start.12
  109.1 72.4 %backward_h.1 = f32[1040,2048]{1,0:T(8,128)} custom-call(f32[12800,1024]{1,0:T(8,128)} %get-tuple-element.29.lg_ref.refs_0_, bf16[12572,2048]{1,0:T(8,128)(2,1)} %e_ref.13, f32[8,1024]{1,0:T(8,128)} %exchange_stats.1.st_ref, f32[1024,1]{1,0:T(8,128)} %get-tuple-element.31.inv_ref, bf16[1024,2048]{1,0:T(8,128)(2,1)} %bitcast.46, f32[1024,2048]{1,0:T(8,128)} %bitcast.42), custom_call_target="tpu_custom_call" | custom-call | flops 52730789888 | bytes 102989824 | tf_op jit(solution)/shard_map/backward_h/pallas_call | solution.py:171
  192.6 5.2 collective-permute-done.12.refs_4_
  199.1 89.2 %collective-permute-done.15.refs_7_ = f32[512,2048]{1,0:T(8,128)} collective-permute-done((f32[512,2048]{1,0:T(8,128)}, f32[512,2048]{1,0:T(8,128)}, u32[]{:S(2)}, u32[]{:S(2)}) %collective-permute-start.15) | collective-permute-done | bytes 4194336 | tf_op jit(solution)/shard_map/ppermute | solution.py:557
  289.3 57.2 %plane_rows.2 = (f32[896,2048]{1,0:T(8,128)}, bf16[7,1024,2048]{2,1,0:T(8,128)(2,1)}, f32[2,1024,2048]{2,1,0:T(8,128)}) custom-call(bf16[12572,2048]{1,0:T(8,128)(2,1)} %e_ref.13, f32[8,8,1024]{2,1,0:T(8,128)} %bitcast_dynamic-update-slice_fusion.st_ref, f32[12800,1024]{1,0:T(8,128)} %get-tuple-element.29.lg_ref.refs_0_, ...), custom_call_target="tpu_custom_call" | custom-call | flops 37580963840 | bytes 62914560 | tf_op jit(solution)/shard_map/plane_rows/pallas_call | solution.py:367
  346.5 44.9 %chip_rows.1.acc_ref = f32[2720,2048]{1,0:T(8,128)} custom-call(s32[5]{0:T(128)} %multiply_add_fusion.off_ref, f32[12800,1024]{1,0:T(8,128)} %get-tuple-element.29.lg_ref.refs_0_, bf16[12572,2048]{1,0:T(8,128)(2,1)} %e_ref.13, f32[8,8,1024]{2,1,0:T(8,128)} %bitcast_dynamic-update-slice_fusion.st_ref, bf16[1024,2048]{1,0:T(8,128)(2,1)} %get-tuple-element.28.h_ref.refs_1_, ...), custom_call_target="tpu_custom_call" | custom-call | flops 34225520640 | bytes 44564480 | tf_op jit(solution)/shard_map/chip_rows/pallas_call | solution.py:390
  391.4 30.2 %plane_rows.3 = (f32[448,2048]{1,0:T(8,128)}, f32[448,2048]{1,0:T(8,128)}, bf16[7,1024,2048]{2,1,0:T(8,128)(2,1)}) custom-call(bf16[12572,2048]{1,0:T(8,128)(2,1)} %e_ref.13, f32[8,8,1024]{2,1,0:T(8,128)} %bitcast_dynamic-update-slice_fusion.st_ref, f32[896,2048]{1,0:T(8,128)} %get-tuple-element.36.refs_0_, ...), custom_call_target="tpu_custom_call", output_to_operand_aliasing={{2}: (3, {})} | custom-call | flops 15032385536 | bytes 25165824 | tf_op jit(solution)/shard_map/plane_rows/pallas_call | solution.py:367
  421.7 1.6 collective-permute-start.21
  424.0 96.4 %rest_rows.2 = (f32[1632,2048]{1,0:T(8,128)}, f32[12572,2048]{1,0:T(8,128)}) custom-call(s32[5]{0:T(128)} %multiply_add_fusion.off_ref, bf16[12572,2048]{1,0:T(8,128)(2,1)} %e_ref.13, f32[8,8,1024]{2,1,0:T(8,128)} %bitcast_dynamic-update-slice_fusion.st_ref, bf16[7,1024,2048]{2,1,0:T(8,128)(2,1)} %get-tuple-element.37.h_ref, f32[2720,2048]{1,0:T(8,128)} %chip_rows.1.acc_ref), custom_call_target="tpu_custom_call" | custom-call | flops 82141249536 | bytes 33423360 | tf_op jit(solution)/shard_map/rest_rows/pallas_call | solution.py:455
  523.2 17.9 %collective-permute-done = f32[24,128]{1,0:T(8,128)S(1)} collective-permute-done((f32[24,128]{1,0:T(8,128)S(1)}, f32[24,128]{1,0:T(8,128)S(1)}, u32[]{:S(2)}, u32[]{:S(2)}) %collective-permute-start) | collective-permute-done | bytes 12320 | tf_op jit(solution)/shard_map/ppermute | solution.py:557
  541.1 2.5 collective-permute-done.1
  545.1 1.7 collective-permute-done.2
  548.9 3.2 collective-permute-start.25
  552.1 67.6 %rest_rows.3 = (f32[1088,2048]{1,0:T(8,128)}, f32[12572,2048]{1,0:T(8,128)}) custom-call(s32[5]{0:T(128)} %multiply_add_fusion.off_ref, bf16[12572,2048]{1,0:T(8,128)(2,1)} %e_ref.13, f32[8,8,1024]{2,1,0:T(8,128)} %bitcast_dynamic-update-slice_fusion.st_ref, bf16[7,1024,2048]{2,1,0:T(8,128)(2,1)} %get-tuple-element.37.h_ref, ...), custom_call_target="tpu_custom_call", output_to_operand_aliasing={{1}: (5, {})} | custom-call | flops 54760833024 | bytes 22282240 | tf_op jit(solution)/shard_map/rest_rows/pallas_call | solution.py:455
  619.7 6.4 collective-permute-done.22.refs_6_
  626.2 3.3 collective-permute-start.27
  629.5 75.1 %collective-permute-done.24.refs_8_ = f32[448,2048]{1,0:T(8,128)} collective-permute-done((f32[448,2048]{1,0:T(8,128)}, f32[448,2048]{1,0:T(8,128)}, u32[]{:S(2)}, u32[]{:S(2)}) %collective-permute-start.24) | collective-permute-done | bytes 3670048 | tf_op jit(solution)/shard_map/ppermute | solution.py:557
  704.6 3.5 collective-permute-start.26
  710.5 4.0 collective-permute-done.26.refs_10_
  714.9 74.5 %collective-permute-done.28.refs_0_ = f32[448,2048]{1,0:T(8,128)} collective-permute-done((f32[448,2048]{1,0:T(8,128)}, f32[448,2048]{1,0:T(8,128)}, u32[]{:S(2)}, u32[]{:S(2)}) %collective-permute-start.28) | collective-permute-done | bytes 3670048 | tf_op jit(solution)/shard_map/ppermute | solution.py:557
  791.8 12.7 %resid_grad.1 = f32[1024,2048]{1,0:T(8,128)} custom-call(f32[1040,2048]{1,0:T(8,128)} %all-reduce.3.cloned.1.call-done.dh_ref, bf16[1024,2048]{1,0:T(8,128)(2,1)} %bitcast.47, f32[1024,2048]{1,0:T(8,128)} %bitcast.43, f32[1024,1]{1,0:T(8,128)} %get-tuple-element.31.inv_ref, f32[1,2048]{1,0:T(1,128)} %bitcast.51), custom_call_target="tpu_custom_call" | custom-call | flops 16777216 | bytes 29360128 | tf_op jit(solution)/shard_map/resid_grad/pallas_call | solution.py:193
  806.5 34.1 %place.4.refs_3_ = f32[12572,2048]{1,0:T(8,128)} custom-call(s32[11]{0:T(128)} %pad_add_fusion.pos_ref, f32[1632,2048]{1,0:T(8,128)} %collective-permute-done.18.refs_0_, f32[448,2048]{1,0:T(8,128)} %get-tuple-element.38.refs_1_, f32[448,2048]{1,0:T(8,128)} %get-tuple-element.41.refs_2_, ...), custom_call_target="tpu_custom_call", output_to_operand_aliasing={{}: (12, {})} | custom-call | flops 1000 | bytes 205979648 | tf_op jit(solution)/shard_map/place/pallas_call | solution.py:528
  840.7 12.3 %place.5.refs_2_ = f32[12572,2048]{1,0:T(8,128)} custom-call(s32[11]{0:T(128)} %pad_add_fusion.pos_ref, f32[1088,2048]{1,0:T(8,128)} %collective-permute-done.27.refs_0_.other_ref, f32[448,2048]{1,0:T(8,128)} %collective-permute-done.32.refs_1_, f32[448,2048]{1,0:T(8,128)} %collective-permute-done.33.refs_2_, ...), custom_call_target="tpu_custom_call", output_to_operand_aliasing={{}: (4, {})} | custom-call | flops 1000 | bytes 205979648 | tf_op jit(solution)/shard_map/place/pallas_call | solution.py:528
  854.2 6.8 place.6.refs_2_
  861.0 6.8 place.7._
  867.8 2.2 place_tail.1
  (83 shorter events, 36.1 us)
Async XLA Ops:
  7.2 513.4 %all-reduce.3.cloned.1.call-start = ((), (), s32[]{:S(2)}) async-start(), calls=%async_computation | async-start | bytes 17039360 | tf_op jit(solution)/shard_map/psum | solution.py:582
  13.6 94.5 %collective-permute-start.10 = (f32[512,2048]{1,0:T(8,128)}, f32[512,2048]{1,0:T(8,128)}, u32[]{:S(2)}, u32[]{:S(2)}) collective-permute-start(f32[512,2048]{1,0:T(8,128)} %get-tuple-element.32), channel_id=1, source_target_pairs={{0,1},{1,0},{2,3},{3,2},{4,5},{5,4},{6,7},{7,6},{8,9},{9,8},{10,11... | collective-permute-start | bytes 12582920 | tf_op jit(solution)/shard_map/ppermute | solution.py:557
  97.2 3.8 collective-permute-start.3
  98.9 4.2 collective-permute-start.5
  100.2 4.4 collective-permute-start.6
  100.9 5.2 collective-permute-start.7
  101.0 5.2 collective-permute-start.8
  103.1 4.6 collective-permute-start.9
  104.6 93.2 %collective-permute-start.12 = (f32[512,2048]{1,0:T(8,128)}, f32[512,2048]{1,0:T(8,128)}, u32[]{:S(2)}, u32[]{:S(2)}) collective-permute-start(f32[512,2048]{1,0:T(8,128)} %get-tuple-element.32), channel_id=1, source_target_pairs={{0,2},{1,3},{2,0},{3,1},{4,6},{5,7},{6,4},{7,5},{8,10},{9,11},{10,... | collective-permute-start | bytes 12582920 | tf_op jit(solution)/shard_map/ppermute | solution.py:557
  106.2 183.1 %collective-permute-start.11 = (f32[512,2048]{1,0:T(8,128)}, f32[512,2048]{1,0:T(8,128)}, u32[]{:S(2)}, u32[]{:S(2)}) collective-permute-start(f32[512,2048]{1,0:T(8,128)} %get-tuple-element.33), channel_id=1, source_target_pairs={{0,1},{1,0},{2,3},{3,2},{4,5},{5,4},{6,7},{7,6},{8,9},{9,8},{10,11... | collective-permute-start | bytes 12582920 | tf_op jit(solution)/shard_map/ppermute | solution.py:557
  106.2 183.1 %collective-permute-start.13 = (f32[512,2048]{1,0:T(8,128)}, f32[512,2048]{1,0:T(8,128)}, u32[]{:S(2)}, u32[]{:S(2)}) collective-permute-start(f32[512,2048]{1,0:T(8,128)} %get-tuple-element.33), channel_id=1, source_target_pairs={{0,2},{1,3},{2,0},{3,1},{4,6},{5,7},{6,4},{7,5},{8,10},{9,11},{10,... | collective-permute-start | bytes 12582920 | tf_op jit(solution)/shard_map/ppermute | solution.py:557
  107.7 181.6 %collective-permute-start.14 = (f32[512,2048]{1,0:T(8,128)}, f32[512,2048]{1,0:T(8,128)}, u32[]{:S(2)}, u32[]{:S(2)}) collective-permute-start(f32[512,2048]{1,0:T(8,128)} %get-tuple-element.32), channel_id=1, source_target_pairs={{0,4},{1,5},{2,6},{3,7},{4,0},{5,1},{6,2},{7,3},{8,12},{9,13},{10,... | collective-permute-start | bytes 12582920 | tf_op jit(solution)/shard_map/ppermute | solution.py:557
  108.1 180.2 %collective-permute-start.15 = (f32[512,2048]{1,0:T(8,128)}, f32[512,2048]{1,0:T(8,128)}, u32[]{:S(2)}, u32[]{:S(2)}) collective-permute-start(f32[512,2048]{1,0:T(8,128)} %get-tuple-element.33), channel_id=1, source_target_pairs={{0,4},{1,5},{2,6},{3,7},{4,0},{5,1},{6,2},{7,3},{8,12},{9,13},{10,... | collective-permute-start | bytes 12582920 | tf_op jit(solution)/shard_map/ppermute | solution.py:557
  197.8 193.6 %collective-permute-start.16 = (f32[512,2048]{1,0:T(8,128)}, f32[512,2048]{1,0:T(8,128)}, u32[]{:S(2)}, u32[]{:S(2)}) collective-permute-start(f32[512,2048]{1,0:T(8,128)} %collective-permute-done.12.refs_4_), channel_id=1, source_target_pairs={{0,4},{1,5},{2,6},{3,7},{4,0},{5,1},{6,2},{7,3},{8,12},{9,13},{10,... | collective-permute-start | bytes 12582920 | tf_op jit(solution)/shard_map/ppermute | solution.py:557
  288.3 103.1 %collective-permute-start.17 = (f32[512,2048]{1,0:T(8,128)}, f32[512,2048]{1,0:T(8,128)}, u32[]{:S(2)}, u32[]{:S(2)}) collective-permute-start(f32[512,2048]{1,0:T(8,128)} %collective-permute-done.15.refs_7_), channel_id=1, source_target_pairs={{0,2},{1,3},{2,0},{3,1},{4,6},{5,7},{6,4},{7,5},{8,10},{9,11},{10,... | collective-permute-start | bytes 12582920 | tf_op jit(solution)/shard_map/ppermute | solution.py:557
  421.6 125.8 %collective-permute-start.19 = (f32[448,2048]{1,0:T(8,128)}, f32[448,2048]{1,0:T(8,128)}, u32[]{:S(2)}, u32[]{:S(2)}) collective-permute-start(f32[448,2048]{1,0:T(8,128)} %get-tuple-element.38.refs_1_), channel_id=1, source_target_pairs={{0,1},{1,0},{2,3},{3,2},{4,5},{5,4},{6,7},{7,6},{8,9},{9,8},{10,11... | collective-permute-start | bytes 11010056 | tf_op jit(solution)/shard_map/ppermute | solution.py:557
  421.7 127.2 %collective-permute-start.21 = (f32[448,2048]{1,0:T(8,128)}, f32[448,2048]{1,0:T(8,128)}, u32[]{:S(2)}, u32[]{:S(2)}) collective-permute-start(f32[448,2048]{1,0:T(8,128)} %get-tuple-element.38.refs_1_), channel_id=1, source_target_pairs={{0,2},{1,3},{2,0},{3,1},{4,6},{5,7},{6,4},{7,5},{8,10},{9,11},{10,... | collective-permute-start | bytes 11010056 | tf_op jit(solution)/shard_map/ppermute | solution.py:557
  423.3 125.0 %collective-permute-start.20 = (f32[448,2048]{1,0:T(8,128)}, f32[448,2048]{1,0:T(8,128)}, u32[]{:S(2)}, u32[]{:S(2)}) collective-permute-start(f32[448,2048]{1,0:T(8,128)} %get-tuple-element.41.refs_2_), channel_id=1, source_target_pairs={{0,1},{1,0},{2,3},{3,2},{4,5},{5,4},{6,7},{7,6},{8,9},{9,8},{10,11... | collective-permute-start | bytes 11010056 | tf_op jit(solution)/shard_map/ppermute | solution.py:557
  520.4 270.7 %collective-permute-start.18 = (f32[1632,2048]{1,0:T(8,128)}, f32[1632,2048]{1,0:T(8,128)}, u32[]{:S(2)}, u32[]{:S(2)}) collective-permute-start(f32[1632,2048]{1,0:T(8,128)} %get-tuple-element.40), channel_id=1, source_target_pairs={{0,1},{1,0},{2,3},{3,2},{4,5},{5,4},{6,7},{7,6},{8,9},{9,8},{10,11... | collective-permute-start | bytes 40108040 | tf_op jit(solution)/shard_map/ppermute | solution.py:557
  522.7 18.4 %collective-permute-start = (f32[24,128]{1,0:T(8,128)S(1)}, f32[24,128]{1,0:T(8,128)S(1)}, u32[]{:S(2)}, u32[]{:S(2)}) collective-permute-start(f32[24,128]{1,0:T(8,128)S(1)} %pad_bitcast_fusion), channel_id=1, source_target_pairs={{0,1},{1,0},{2,3},{3,2},{4,5},{5,4},{6,7},{7,6},{8,9},{9,8},{10,11... | collective-permute-start | bytes 36872 | tf_op jit(solution)/shard_map/ppermute | solution.py:557
  547.4 78.8 %collective-permute-start.22 = (f32[448,2048]{1,0:T(8,128)}, f32[448,2048]{1,0:T(8,128)}, u32[]{:S(2)}, u32[]{:S(2)}) collective-permute-start(f32[448,2048]{1,0:T(8,128)} %get-tuple-element.41.refs_2_), channel_id=1, source_target_pairs={{0,2},{1,3},{2,0},{3,1},{4,6},{5,7},{6,4},{7,5},{8,10},{9,11},{10,... | collective-permute-start | bytes 11010056 | tf_op jit(solution)/shard_map/ppermute | solution.py:557
  547.4 160.7 %collective-permute-start.23 = (f32[448,2048]{1,0:T(8,128)}, f32[448,2048]{1,0:T(8,128)}, u32[]{:S(2)}, u32[]{:S(2)}) collective-permute-start(f32[448,2048]{1,0:T(8,128)} %get-tuple-element.38.refs_1_), channel_id=1, source_target_pairs={{0,4},{1,5},{2,6},{3,7},{4,0},{5,1},{6,2},{7,3},{8,12},{9,13},{10,... | collective-permute-start | bytes 11010056 | tf_op jit(solution)/shard_map/ppermute | solution.py:557
  548.3 156.3 %collective-permute-start.24 = (f32[448,2048]{1,0:T(8,128)}, f32[448,2048]{1,0:T(8,128)}, u32[]{:S(2)}, u32[]{:S(2)}) collective-permute-start(f32[448,2048]{1,0:T(8,128)} %get-tuple-element.41.refs_2_), channel_id=1, source_target_pairs={{0,4},{1,5},{2,6},{3,7},{4,0},{5,1},{6,2},{7,3},{8,12},{9,13},{10,... | collective-permute-start | bytes 11010056 | tf_op jit(solution)/shard_map/ppermute | solution.py:557
  548.9 160.1 %collective-permute-start.25 = (f32[448,2048]{1,0:T(8,128)}, f32[448,2048]{1,0:T(8,128)}, u32[]{:S(2)}, u32[]{:S(2)}) collective-permute-start(f32[448,2048]{1,0:T(8,128)} %collective-permute-done.21.refs_5_), channel_id=1, source_target_pairs={{0,1},{1,0},{2,3},{3,2},{4,5},{5,4},{6,7},{7,6},{8,9},{9,8},{10,11... | collective-permute-start | bytes 11010056 | tf_op jit(solution)/shard_map/ppermute | solution.py:557
  626.2 214.5 %collective-permute-start.27 = (f32[1088,2048]{1,0:T(8,128)}, f32[1088,2048]{1,0:T(8,128)}, u32[]{:S(2)}, u32[]{:S(2)}) collective-permute-start(f32[1088,2048]{1,0:T(8,128)} %get-tuple-element.46.own_ref), channel_id=1, source_target_pairs={{0,1},{1,0},{2,3},{3,2},{4,5},{5,4},{6,7},{7,6},{8,9},{9,8},{10,11... | collective-permute-start | bytes 26738696 | tf_op jit(solution)/shard_map/ppermute | solution.py:557
  704.6 9.9 %collective-permute-start.26 = (f32[448,2048]{1,0:T(8,128)}, f32[448,2048]{1,0:T(8,128)}, u32[]{:S(2)}, u32[]{:S(2)}) collective-permute-start(f32[448,2048]{1,0:T(8,128)} %collective-permute-done.24.refs_8_), channel_id=1, source_target_pairs={{0,1},{1,0},{2,3},{3,2},{4,5},{5,4},{6,7},{7,6},{8,9},{9,8},{10,11... | collective-permute-start | bytes 11010056 | tf_op jit(solution)/shard_map/ppermute | solution.py:557
  708.1 81.2 %collective-permute-start.28 = (f32[448,2048]{1,0:T(8,128)}, f32[448,2048]{1,0:T(8,128)}, u32[]{:S(2)}, u32[]{:S(2)}) collective-permute-start(f32[448,2048]{1,0:T(8,128)} %collective-permute-done.21.refs_5_), channel_id=1, source_target_pairs={{0,4},{1,5},{2,6},{3,7},{4,0},{5,1},{6,2},{7,3},{8,12},{9,13},{10,... | collective-permute-start | bytes 11010056 | tf_op jit(solution)/shard_map/ppermute | solution.py:557
  709.0 81.2 %collective-permute-start.30 = (f32[448,2048]{1,0:T(8,128)}, f32[448,2048]{1,0:T(8,128)}, u32[]{:S(2)}, u32[]{:S(2)}) collective-permute-start(f32[448,2048]{1,0:T(8,128)} %collective-permute-done.24.refs_8_), channel_id=1, source_target_pairs={{0,2},{1,3},{2,0},{3,1},{4,6},{5,7},{6,4},{7,5},{8,10},{9,11},{10,... | collective-permute-start | bytes 11010056 | tf_op jit(solution)/shard_map/ppermute | solution.py:557
  714.5 126.1 %collective-permute-start.32 = (f32[448,2048]{1,0:T(8,128)}, f32[448,2048]{1,0:T(8,128)}, u32[]{:S(2)}, u32[]{:S(2)}) collective-permute-start(f32[448,2048]{1,0:T(8,128)} %collective-permute-done.22.refs_6_), channel_id=1, source_target_pairs={{0,1},{1,0},{2,3},{3,2},{4,5},{5,4},{6,7},{7,6},{8,9},{9,8},{10,11... | collective-permute-start | bytes 11010056 | tf_op jit(solution)/shard_map/ppermute | solution.py:557
  789.3 51.3 %collective-permute-start.33 = (f32[448,2048]{1,0:T(8,128)}, f32[448,2048]{1,0:T(8,128)}, u32[]{:S(2)}, u32[]{:S(2)}) collective-permute-start(f32[448,2048]{1,0:T(8,128)} %collective-permute-done.23.refs_7_), channel_id=1, source_target_pairs={{0,1},{1,0},{2,3},{3,2},{4,5},{5,4},{6,7},{7,6},{8,9},{9,8},{10,11... | collective-permute-start | bytes 11010056 | tf_op jit(solution)/shard_map/ppermute | solution.py:557
  790.2 70.8 %collective-permute-start.29 = (f32[448,2048]{1,0:T(8,128)}, f32[448,2048]{1,0:T(8,128)}, u32[]{:S(2)}, u32[]{:S(2)}) collective-permute-start(f32[448,2048]{1,0:T(8,128)} %collective-permute-done.28.refs_0_), channel_id=1, source_target_pairs={{0,1},{1,0},{2,3},{3,2},{4,5},{5,4},{6,7},{7,6},{8,9},{9,8},{10,11... | collective-permute-start | bytes 11010056 | tf_op jit(solution)/shard_map/ppermute | solution.py:557
  791.1 69.9 %collective-permute-start.31 = (f32[448,2048]{1,0:T(8,128)}, f32[448,2048]{1,0:T(8,128)}, u32[]{:S(2)}, u32[]{:S(2)}) collective-permute-start(f32[448,2048]{1,0:T(8,128)} %collective-permute-done.30.refs_1_), channel_id=1, source_target_pairs={{0,1},{1,0},{2,3},{3,2},{4,5},{5,4},{6,7},{7,6},{8,9},{9,8},{10,11... | collective-permute-start | bytes 11010056 | tf_op jit(solution)/shard_map/ppermute | solution.py:557
  (7 other events, 10.9 us)
Sparse Core Ops, SparseCore 0:
  181.7 296.1 all-reduce.2
